TPU v7x, 256 devices: a whole 4x4x8 slice. The times are simulated.
256 devices in a mesh: group: 16 (over z, x_lo), slot: 16 (over y, x_hi, core).
Axes of the slice: x: 4 (x_hi: 2, x_lo: 2; x = x_hi * 2 + x_lo), y: 4, z: 8, core: 2. Of those that a mesh axis runs over, the one named last changes fastest.
Arguments:
- rows_in: bfloat16 [131072, 768], P(('group', 'slot')), may hold values from -6 to 6
- cotangent: bfloat16 [131072, 2048], P(('group', 'slot')), may hold values from -6 to 6
- gate_prob: float32 [131072], P(('group', 'slot')), may hold values from 0.05 to 0.5
- row_counts: int32 [256], P(('group', 'slot')), may hold values from 1 to 512
- old_place: int32 [256, 1], replicated, may hold values from 0 to 63
- new_place: int32 [256, 1], replicated, may hold values from 0 to 63
- rows_next: bfloat16 [131072, 768], P(('group', 'slot')), may hold values from -6 to 6
- master: float32 [64, 768, 2048], P(None, 'slot', 'group'), may hold values from -0.21875 to 0.21875
- moment_one: bfloat16 [64, 768, 2048], P(None, 'slot', 'group'), may hold values from -18 to 18
- moment_two: bfloat16 [64, 768, 2048], P(None, 'slot', 'group'), may hold values from 0.049804688 to 2
Outputs:
- input_grad: bfloat16 [131072, 768], P(('group', 'slot'))
- gate_grad: float32 [131072], P(('group', 'slot'))
- new_master: float32 [64, 768, 2048], P(None, 'slot', 'group')
- new_first: bfloat16 [64, 768, 2048], P(None, 'slot', 'group')
- new_second: bfloat16 [64, 768, 2048], P(None, 'slot', 'group')
- next_out: bfloat16 [131072, 2048], P(('group', 'slot'))
Inputs may be any that keep to these rules, and one draw needn't show every extreme that they name: `old_place`: every one of the 64 experts is held by at least one of the 256 slots. `new_place`: every one of the 64 experts is listed for at least one of the 256 slots.
All inputs are finite; a program needn't handle non-finite values.
Results may differ from a plain program's by a relative error of at most 0.004.
The roundings to bfloat16 on the way count: a program that leaves them out, or rounds other values in their place, can miss the bound.
Values may be sent and summed in bfloat16 or wider, within the bound.
A program may use at most 128 MiB of HBM per device.

v0:
```python
import jax
import jax.numpy as jnp
from jax import lax
from jax.sharding import PartitionSpec as P

beta_one = 0.9
beta_two = 0.999
adam_eps = 1e-08
learn_rate = 0.006
fix_one = 0.9999734386011124
fix_two = 0.0952078528862904


def cut_along(x, dim, peers):
    before, after = (x.shape[:dim], x.shape[dim + 1 :])
    return jnp.moveaxis(x.reshape(*before, peers, -1, *after), dim, 0)


def joined_along(parts, dim):
    lengths = list(parts.shape[1:])
    lengths[dim] *= parts.shape[0]
    return jnp.moveaxis(parts, 0, dim).reshape(lengths)


def exchange_both(x, axis, axes, splits, concats):
    sizes = [lax.axis_size(a) for a in axes]
    parts = cut_along(x, splits[0], sizes[0])
    parts = jnp.moveaxis(cut_along(parts, splits[1] + 1, sizes[1]), 0, 1)
    inside = parts.shape[2:]
    parts = parts.reshape(-1, *inside)
    parts = lax.all_to_all(parts, axis, split_axis=0, concat_axis=0, tiled=True)
    parts = joined_along(parts.reshape(*sizes, *inside), concats[0] + 1)
    return joined_along(parts, concats[1])


def to_slots(shard_in, expert_of, slot_count, group_count):
    part_rows = shard_in.shape[1]
    part_cols = shard_in.shape[2]
    picked = shard_in[expert_of].astype(jnp.bfloat16)
    picked = picked.reshape(group_count, slot_count, part_rows, part_cols)
    buffer = jnp.transpose(picked, (1, 2, 0, 3))
    arrived = exchange_both(buffer, ("group", "slot"), ("group", "slot"), (2, 0), (2, 0))
    return arrived.reshape(slot_count * part_rows, group_count * part_cols)


def shards(
    rows_in,
    cotangent,
    gate_prob,
    row_counts,
    old_place,
    new_place,
    rows_next,
    master,
    moment_one,
    moment_two,
):
    slot_count = lax.axis_size("slot")
    group_count = lax.axis_size("group")
    row_count = rows_in.shape[0]
    part_rows = master.shape[1]
    part_cols = master.shape[2]
    expert_of = old_place[:, 0]
    weight = to_slots(master, expert_of, slot_count, group_count)
    live_rows = (jnp.arange(row_count, dtype=jnp.int32) < row_counts[0])[:, None]
    masked_in = jnp.where(live_rows, rows_in, jnp.zeros_like(rows_in))
    masked_out = jnp.where(live_rows, cotangent, jnp.zeros_like(cotangent))
    back_prod = lax.dot_general(
        masked_out, weight, (((1,), (1,)), ((), ())), preferred_element_type=jnp.float32
    )
    input_grad = (gate_prob[:, None] * back_prod).astype(jnp.bfloat16)
    forward_out = jnp.dot(masked_in, weight, preferred_element_type=jnp.float32)
    gate_grad = jnp.sum(masked_out.astype(jnp.float32) * forward_out, axis=1)
    scaled_out = (gate_prob[:, None] * masked_out.astype(jnp.float32)).astype(jnp.bfloat16)
    expert_ids = jnp.arange(master.shape[0], dtype=jnp.int32)
    owner_map = (
        expert_of.reshape(group_count, slot_count)[None, :, :] == expert_ids[:, None, None]
    ).astype(jnp.bfloat16)
    slot_grad = lax.dot_general(
        masked_in, scaled_out, (((0,), (0,)), ((), ())), preferred_element_type=jnp.float32
    ).astype(jnp.bfloat16)
    buffer = slot_grad.reshape(slot_count, part_rows, group_count, part_cols)
    arrived = exchange_both(buffer, ("group", "slot"), ("group", "slot"), (2, 0), (2, 0))
    grad_sum = jnp.einsum("egs,sfgd->efd", owner_map, arrived, preferred_element_type=jnp.float32)
    first_full = beta_one * moment_one.astype(jnp.float32) + (1.0 - beta_one) * grad_sum
    second_full = beta_two * moment_two.astype(jnp.float32) + (1.0 - beta_two) * grad_sum * grad_sum
    new_master = master - learn_rate * (first_full / fix_one) / (
        jnp.sqrt(second_full / fix_two) + adam_eps
    )
    weight_next = to_slots(new_master, new_place[:, 0], slot_count, group_count)
    next_out = jnp.dot(rows_next, weight_next, preferred_element_type=jnp.float32).astype(
        jnp.bfloat16
    )
    return (
        input_grad,
        gate_grad,
        new_master,
        first_full.astype(jnp.bfloat16),
        second_full.astype(jnp.bfloat16),
        next_out,
    )


def solution(mesh):
    in_specs = (
        P(("group", "slot"), None),
        P(("group", "slot"), None),
        P(("group", "slot")),
        P(("group", "slot")),
        P(),
        P(),
        P(("group", "slot"), None),
        P(None, "slot", "group"),
        P(None, "slot", "group"),
        P(None, "slot", "group"),
    )
    out_specs = (
        P(("group", "slot"), None),
        P(("group", "slot")),
        P(None, "slot", "group"),
        P(None, "slot", "group"),
        P(None, "slot", "group"),
        P(("group", "slot"), None),
    )
    return jax.shard_map(shards, mesh=mesh, in_specs=in_specs, out_specs=out_specs, check_vma=False)
```

profile of v0, /device:TPU:1, one launch (start us, length us, event | category | flops | bytes accessed | tf_op | source)
XLA Modules:
  0.0 272.7 jit_solution(11082064156369949860)
XLA Ops:
  0.6 0.0 copy-start
  1.4 3.9 %fusion.18 = bf16[96,8,16,128]{3,1,2,0:T(8,128)(2,1)S(1)} fusion(f32[512]{0:T(512)} %param.12, bf16[512,768]{1,0:T(8,128)(2,1)} %param.10, pred[512]{0:T(512)(128)(4,1)S(1)} %iota_compare_fusion.1, bf16[512,2048]{1,0:T(8,128)(2,1)} %param.11), kind=kOutput, calls=%fused_computation.22 | convolution fusion | flops 1616773120 | bytes 6031872 | tf_op jit(solution)/shard_map/dot_general | solution.py:79
  5.3 1.0 copy.60
  6.3 2.5 copy.47
  8.8 0.0 copy-start.4
  8.8 0.0 copy-start.2
  8.8 16.5 %all-to-all-start.1 = ((bf16[256,1,48,1,128]{4,2,3,1,0:T(8,128)(2,1)}), bf16[256,1,48,1,128]{4,2,3,1,0:T(8,128)(2,1)}, u32[]{:S(2)}, u32[]{:S(2)}) async-start(bf16[256,1,48,1,128]{4,2,3,1,0:T(8,128)(2,1)} %bitcast.91), calls=%async_computation.1 | async-start | bytes 6291456 | tf_op jit(solution)/shard_map/all_to_all | solution.py:31
  25.3 0.5 broadcast.35
  25.8 0.0 copy-done.4
  25.8 0.7 fusion.33
  26.5 0.0 copy-done.2
  26.5 2.8 %gather_fusion = bf16[256,48,128]{2,1,0:T(8,128)(2,1)} fusion(f32[64,48,128]{2,1,0:T(8,128)S(1)} %copy-done.2, s32[1024]{0:T(1024)S(1)} %pad_clamp_fusion.1), kind=kCustom, calls=%fused_computation | custom fusion | bytes 6292480 | tf_op jit(solution)/shard_map/gather | solution.py:39
  29.3 70.7 %all-to-all-done.1 = bf16[256,1,48,1,128]{4,2,3,1,0:T(8,128)(2,1)} async-done(((bf16[256,1,48,1,128]{4,2,3,1,0:T(8,128)(2,1)}), bf16[256,1,48,1,128]{4,2,3,1,0:T(8,128)(2,1)}, u32[]{:S(2)}, u32[]{:S(2)}) %all-to-all-start.1) | async-done | bytes 3145760 | tf_op jit(solution)/shard_map/all_to_all | solution.py:31
  100.0 0.0 copy-start.5
  100.0 7.5 %all-to-all-start = ((bf16[256,1,48,1,128]{4,2,3,1,0:T(8,128)(2,1)}), bf16[256,1,48,1,128]{4,2,3,1,0:T(8,128)(2,1)}, u32[]{:S(2)}, u32[]{:S(2)}) async-start(bf16[256,1,48,1,128]{4,2,3,1,0:T(8,128)(2,1)} %bitcast.93), calls=%async_computation | async-start | bytes 6291456 | tf_op jit(solution)/shard_map/all_to_all | solution.py:31
  107.5 0.1 eq.15
  107.6 0.0 copy-done.5
  107.6 0.0 copy-start.7
  107.6 0.0 copy-start.8
  107.7 2.8 %copy.49 = bf16[256,1,48,1,128]{4,0,2,3,1:T(8,128)(2,1)S(1)} copy(bf16[256,1,48,1,128]{4,2,3,1,0:T(8,128)(2,1)} %all-to-all-done.1) | data formatting | bytes 6291456 | tf_op jit(solution)/shard_map/all_to_all | solution.py:31
  110.5 0.0 copy-done.7
  110.5 0.0 copy-done.8
  110.5 2.8 %fusion.26 = (bf16[64,48,128]{2,0,1:T(8,128)(2,1)}, f32[64,48,128]{2,0,1:T(8,128)S(1)}, bf16[64,48,128]{2,0,1:T(8,128)(2,1)S(1)}) fusion(bf16[64,48,128]{2,1,0:T(8,128)(2,1)S(1)} %copy-done.7, bf16[64,48,128]{2,1,0:T(8,128)(2,1)S(1)} %copy-done.8, f32[64,48,128]{2,1,0:T(8,128)S(1)} %copy-done.2, bf16[16,48,16,128]{3,0,2,1:T(8,128)(2,1)S(1)} %bitcast.97, ...), kind=kOutput, calls=%fused_computation.29 | convolution fusion | flops 207634432 | bytes 9438208 | tf_op jit(solution)/shard_map/egs,sfgd->efd/dot_general | solution.py:84
  113.3 0.9 copy.54
  114.2 0.0 copy-start.1
  114.2 2.9 %gather_fusion.1 = bf16[256,48,128]{2,1,0:T(8,128)(2,1)} fusion(f32[64,48,128]{2,1,0:T(8,128)S(1)} %copy.54, s32[1024]{0:T(1024)S(1)} %pad_clamp_fusion), kind=kCustom, calls=%fused_computation.1 | custom fusion | bytes 6292480 | tf_op jit(solution)/shard_map/gather | solution.py:39
  117.1 0.0 copy-done.1
  117.1 65.1 %all-to-all-done = bf16[256,1,48,1,128]{4,2,3,1,0:T(8,128)(2,1)} async-done(((bf16[256,1,48,1,128]{4,2,3,1,0:T(8,128)(2,1)}), bf16[256,1,48,1,128]{4,2,3,1,0:T(8,128)(2,1)}, u32[]{:S(2)}, u32[]{:S(2)}) %all-to-all-start) | async-done | bytes 3145760 | tf_op jit(solution)/shard_map/all_to_all | solution.py:31
  182.2 7.5 %all-to-all-start.2 = ((bf16[256,1,48,1,128]{4,2,3,1,0:T(8,128)(2,1)}), bf16[256,1,48,1,128]{4,2,3,1,0:T(8,128)(2,1)}, u32[]{:S(2)}, u32[]{:S(2)}) async-start(bf16[256,1,48,1,128]{4,2,3,1,0:T(8,128)(2,1)} %bitcast.94), calls=%async_computation.2 | async-start | bytes 6291456 | tf_op jit(solution)/shard_map/all_to_all | solution.py:31
  189.8 0.0 copy-start.3
  189.8 4.0 %copy.45 = bf16[16,1,48,16,1,128]{5,3,2,0,4,1:T(8,128)(2,1)S(1)} copy(bf16[16,1,48,16,1,128]{5,2,0,3,4,1:T(8,128)(2,1)} %bitcast.8) | data formatting | bytes 6291456 | tf_op jit(solution)/shard_map/transpose | solution.py:22
  193.8 0.0 copy-start.6
  193.8 0.0 copy-start.10
  193.8 0.0 copy-done.3
  193.8 1.4 copy.56
  195.2 1.4 copy.55
  196.6 0.0 copy-done.6
  196.6 0.0 copy-done.10
  196.6 0.0 copy-start.9
  196.6 2.8 %multiply_convert_fusion = bf16[512,768]{1,0:T(8,128)(2,1)} fusion(bf16[96,8,16,128]{3,2,1,0:T(8,128)(2,1)S(1)} %bitcast.95, f32[512]{0:T(512)S(1)} %copy-done.10, bf16[512,2048]{1,0:T(8,128)(2,1)S(1)} %copy-done.6, pred[512]{0:T(512)(128)(4,1)S(1)} %iota_compare_fusion.1), kind=kOutput, calls=%fused_computation.27 | convolution fusion | flops 1612447744 | bytes 6031872 | tf_op jit(solution)/shard_map/dot_general | solution.py:68
  199.3 0.0 copy-done.9
  199.3 2.6 fusion
  202.0 62.5 %all-to-all-done.2 = bf16[256,1,48,1,128]{4,2,3,1,0:T(8,128)(2,1)} async-done(((bf16[256,1,48,1,128]{4,2,3,1,0:T(8,128)(2,1)}), bf16[256,1,48,1,128]{4,2,3,1,0:T(8,128)(2,1)}, u32[]{:S(2)}, u32[]{:S(2)}) %all-to-all-start.2) | async-done | bytes 3145760 | tf_op jit(solution)/shard_map/all_to_all | solution.py:31
  264.5 3.9 %copy.53 = bf16[16,1,48,16,1,128]{5,3,2,0,4,1:T(8,128)(2,1)S(1)} copy(bf16[16,1,48,16,1,128]{5,2,0,3,4,1:T(8,128)(2,1)} %bitcast.25) | data formatting | bytes 6291456 | tf_op jit(solution)/shard_map/transpose | solution.py:22
  268.4 0.0 copy-done
  268.4 2.0 fusion.13
  270.4 2.4 copy.57
  (4 shorter events, 0.0 us)
Async XLA Ops:
  0.6 267.7 %copy-start = (bf16[512,768]{1,0:T(8,128)(2,1)S(1)}, bf16[512,768]{1,0:T(8,128)(2,1)}, u32[]{:S(2)}) copy-start(bf16[512,768]{1,0:T(8,128)(2,1)} %param.16) | copy-start | bytes 2359300
  8.8 17.0 %copy-start.4 = (s32[256,1]{0,1:T(1,128)S(1)}, s32[256,1]{0,1:T(1,128)}, u32[]{:S(2)}) copy-start(s32[256,1]{0,1:T(1,128)} %param.14) | copy-start | bytes 3076
  8.8 17.7 %copy-start.2 = (f32[64,48,128]{2,1,0:T(8,128)S(1)}, f32[64,48,128]{2,1,0:T(8,128)}, u32[]{:S(2)}) copy-start(f32[64,48,128]{2,1,0:T(8,128)} %param.17) | copy-start | bytes 4718596
  8.8 91.2 %all-to-all-start.1 = ((bf16[256,1,48,1,128]{4,2,3,1,0:T(8,128)(2,1)}), bf16[256,1,48,1,128]{4,2,3,1,0:T(8,128)(2,1)}, u32[]{:S(2)}, u32[]{:S(2)}) async-start(bf16[256,1,48,1,128]{4,2,3,1,0:T(8,128)(2,1)} %bitcast.91), calls=%async_computation.1 | async-start | bytes 6291456 | tf_op jit(solution)/shard_map/all_to_all | solution.py:31
  100.0 7.6 %copy-start.5 = (s32[256,1]{0,1:T(1,128)S(1)}, s32[256,1]{0,1:T(1,128)}, u32[]{:S(2)}) copy-start(s32[256,1]{0,1:T(1,128)} %param.15) | copy-start | bytes 3076
  100.0 82.2 %all-to-all-start = ((bf16[256,1,48,1,128]{4,2,3,1,0:T(8,128)(2,1)}), bf16[256,1,48,1,128]{4,2,3,1,0:T(8,128)(2,1)}, u32[]{:S(2)}, u32[]{:S(2)}) async-start(bf16[256,1,48,1,128]{4,2,3,1,0:T(8,128)(2,1)} %bitcast.93), calls=%async_computation | async-start | bytes 6291456 | tf_op jit(solution)/shard_map/all_to_all | solution.py:31
  107.6 2.8 %copy-start.7 = (bf16[64,48,128]{2,1,0:T(8,128)(2,1)S(1)}, bf16[64,48,128]{2,1,0:T(8,128)(2,1)}, u32[]{:S(2)}) copy-start(bf16[64,48,128]{2,1,0:T(8,128)(2,1)} %param.19) | copy-start | bytes 2359300
  107.6 2.8 %copy-start.8 = (bf16[64,48,128]{2,1,0:T(8,128)(2,1)S(1)}, bf16[64,48,128]{2,1,0:T(8,128)(2,1)}, u32[]{:S(2)}) copy-start(bf16[64,48,128]{2,1,0:T(8,128)(2,1)} %param.18) | copy-start | bytes 2359300
  114.2 2.9 %copy-start.1 = (f32[64,48,128]{2,1,0:T(8,128)}, f32[64,48,128]{2,1,0:T(8,128)S(1)}, u32[]{:S(2)}) copy-start(f32[64,48,128]{2,1,0:T(8,128)S(1)} %copy.54) | copy-start | bytes 4718596
  182.2 82.2 %all-to-all-start.2 = ((bf16[256,1,48,1,128]{4,2,3,1,0:T(8,128)(2,1)}), bf16[256,1,48,1,128]{4,2,3,1,0:T(8,128)(2,1)}, u32[]{:S(2)}, u32[]{:S(2)}) async-start(bf16[256,1,48,1,128]{4,2,3,1,0:T(8,128)(2,1)} %bitcast.94), calls=%async_computation.2 | async-start | bytes 6291456 | tf_op jit(solution)/shard_map/all_to_all | solution.py:31
  189.8 4.0 %copy-start.3 = (bf16[64,48,128]{2,0,1:T(8,128)(2,1)S(1)}, bf16[64,48,128]{2,0,1:T(8,128)(2,1)}, u32[]{:S(2)}) copy-start(bf16[64,48,128]{2,0,1:T(8,128)(2,1)} %get-tuple-element.30) | copy-start | bytes 2359300
  193.8 2.8 %copy-start.6 = (bf16[512,2048]{1,0:T(8,128)(2,1)S(1)}, bf16[512,2048]{1,0:T(8,128)(2,1)}, u32[]{:S(2)}) copy-start(bf16[512,2048]{1,0:T(8,128)(2,1)} %param.11) | copy-start | bytes 6291460
  193.8 2.8 %copy-start.10 = (f32[512]{0:T(512)S(1)}, f32[512]{0:T(512)}, u32[]{:S(2)}) copy-start(f32[512]{0:T(512)} %param.12) | copy-start | bytes 6148
  196.6 2.8 %copy-start.9 = (bf16[512,768]{1,0:T(8,128)(2,1)S(1)}, bf16[512,768]{1,0:T(8,128)(2,1)}, u32[]{:S(2)}) copy-start(bf16[512,768]{1,0:T(8,128)(2,1)} %param.10) | copy-start | bytes 2359300
where the time goes:
time: 273 us
  waiting for transfers between devices  198 us (73%)
  starting transfers between devices  31.6 us (12%)
  local copies, waits for them, and re-layouts  26.6 us (10%)
  matrix products  14.1 us (5%)
    all_to_all x3, waiting for transfers between devices, exchange_both(): parts = lax.all_to_all(parts, axis, split_axis=0, concat_axis=0, tiled=True)  198 us
    all_to_all x3, starting transfers between devices, exchange_both(): parts = lax.all_to_all(parts, axis, split_axis=0, concat_axis=0, tiled=True)  31.6 us
    transpose x2, local copies, waits for them, and re-layouts, joined_along(): return jnp.moveaxis(parts, 0, dim).reshape(lengths)  7.9 us
    unnamed x28, local copies, waits for them, and re-layouts  7.66 us
    gather x2, local copies, waits for them, and re-layouts, to_slots(): picked = shard_in[expert_of].astype(jnp.bfloat16)  5.7 us
  transfers between devices with their start and end apart: 3, of which 3 were waited for; matrix products, arithmetic and copies ran while one was open for 9% of the time, Pallas kernels for 0%

commit v1 on v0

v1 whole, which is shorter than its diff:
```python
import functools

import jax
import jax.numpy as jnp
from jax import lax
from jax.experimental import pallas as pl
from jax.experimental.pallas import tpu as pltpu
from jax.sharding import PartitionSpec as P

beta_one = 0.9
beta_two = 0.999
adam_eps = 1e-08
learn_rate = 0.006
fix_one = 0.9999734386011124
fix_two = 0.0952078528862904

EXPERTS = 64
PR = 48
PC = 128
PLANES = 8
INPLANE = 32
FAR = 80
MESH = pl.DeviceIdType.MESH

PREV_AT = 256
LAST_AT = PREV_AT + 2 * FAR
TABLE = LAST_AT + 3 * EXPERTS


def my_place():
    g = lax.axis_index("group")
    s = lax.axis_index("slot")
    z = lax.div(g, 2)
    return z, lax.rem(g, 2) * 16 + s, g, s


def plane_at(z, k):
    return lax.rem(z + (k + PLANES), PLANES)


def device_at(plane, i):
    return (plane * 2 + lax.div(i, 16), lax.rem(i, 16))


def shard_slice(ref, block_row, block_col):
    return ref.at[
        pl.ds(pl.multiple_of(block_row * PR, 16), PR), pl.ds(pl.multiple_of(block_col * PC, PC), PC)
    ]


def send(src, dst, send_sem, recv_sem, device):
    copy = pltpu.make_async_remote_copy(
        src_ref=src,
        dst_ref=dst,
        send_sem=send_sem,
        recv_sem=recv_sem,
        device_id=device,
        device_id_type=MESH,
    )
    copy.start()


def take(ref, sem):
    pltpu.make_async_copy(ref, ref, sem).wait()


class Spread:
    def __init__(self, place, own, weight, near, far, picks, ring_sems, out_sem, in_sems):
        self.place, self.own, self.weight = place, own, weight
        self.near, self.far, self.picks = near, far, picks
        self.ring_sems, self.out_sem, self.in_sems = ring_sems, out_sem, in_sems
        self.z, self.i, self.g, self.s = my_place()
        self.xlo = lax.rem(self.g, 2)

    def ring(self, src, dst, hop, side):
        send(
            src,
            dst,
            self.ring_sems.at[0, hop, side],
            self.ring_sems.at[1, hop, side],
            device_at(plane_at(self.z, 1 - 2 * side), self.i),
        )

    def start_own(self):
        for side in range(2):
            self.ring(self.own, self.near[side], 0, side)

    def wait_near(self, side):
        take(self.near[side], self.ring_sems.at[1, 0, side])

    def forward(self, side):
        self.ring(self.near[side], self.far[side], 1, side)

    def wait_far(self, side):
        take(self.far[side], self.ring_sems.at[1, 1, side])

    def inplane(self, ref, base, k):
        z, i = self.z, self.i
        column = plane_at(z, k) * 2 + self.xlo

        def pick(j, _):
            t = lax.rem(i + j, INPLANE)
            self.picks[base + j] = ref[self.place[z * INPLANE + t]]
            return 0

        def go(j, _):
            t = lax.rem(i + j, INPLANE)
            send(
                self.picks.at[base + j],
                shard_slice(self.weight, self.s, column),
                self.out_sem,
                self.in_sems.at[k + 3],
                device_at(z, t),
            )
            return 0

        lax.fori_loop(0, INPLANE, pick, 0)
        lax.fori_loop(1, INPLANE, go, 0)
        rows = pl.ds(pl.multiple_of(self.s * PR, 16), PR)
        cols = pl.ds(pl.multiple_of(column * PC, PC), PC)
        self.weight[rows, cols] = self.picks[base]

    def outplane(self, side, base):
        ref = self.far[side]
        sign = 1 - 2 * side
        z, i = self.z, self.i
        column = plane_at(z, -2 * sign) * 2 + self.xlo
        one, two = plane_at(z, sign), plane_at(z, 2 * sign)

        def other(j):
            return lax.rem((lax.div(i, 2) + j) * 2, INPLANE) + side

        def pick_one(j, _):
            t = lax.rem(i + j, INPLANE)
            self.picks[base + j] = ref[self.place[one * INPLANE + t]]
            return 0

        def pick_two(j, _):
            self.picks[base + 32 + j] = ref[self.place[two * INPLANE + other(j)]]
            return 0

        def go_one(j, _):
            t = lax.rem(i + j, INPLANE)
            send(
                self.picks.at[base + j],
                shard_slice(self.weight, self.s, column),
                self.out_sem,
                self.in_sems.at[3 - 3 * sign],
                device_at(one, t),
            )
            return 0

        def go_two(j, _):
            send(
                self.picks.at[base + 32 + j],
                shard_slice(self.weight, self.s, column),
                self.out_sem,
                self.in_sems.at[7],
                device_at(two, other(j)),
            )
            return 0

        lax.fori_loop(0, 16, pick_two, 0)
        lax.fori_loop(0, INPLANE, pick_one, 0)
        lax.fori_loop(0, 16, go_two, 0)
        lax.fori_loop(0, INPLANE, go_one, 0)

    def finish(self):
        for k in range(-3, 5):
            count = 31 if -2 <= k <= 2 else 32
            take(self.picks.at[pl.ds(0, count)], self.in_sems.at[k + 3])
        sent = 5 * 31 + 2 * 48
        take(self.picks.at[pl.ds(0, sent)], self.out_sem)
        for hop in range(2):
            for side in range(2):
                take(self.own, self.ring_sems.at[0, hop, side])


SPREAD_SCRATCH = [
    pltpu.VMEM((EXPERTS, PR, PC), jnp.bfloat16),
    pltpu.VMEM((EXPERTS, PR, PC), jnp.bfloat16),
    pltpu.VMEM((EXPERTS, PR, PC), jnp.bfloat16),
    pltpu.VMEM((EXPERTS, PR, PC), jnp.bfloat16),
    pltpu.VMEM((256, PR, PC), jnp.bfloat16),
    pltpu.SemaphoreType.DMA((2, 2, 2)),
    pltpu.SemaphoreType.DMA,
    pltpu.SemaphoreType.DMA((8,)),
]


class Gather:
    def __init__(self, table, grad, total, met0, met1, met2, sums, parts, sems, part_sems):
        self.table, self.grad, self.total = table, grad, total
        self.met0, self.met1, self.met2 = met0, met1, met2
        self.sums = sums
        self.parts = parts
        self.sems, self.part_sems = sems, part_sems
        self.z, self.i, self.g, self.s = my_place()
        self.out_sem = sems.at[0]

    def piece(self, plane, t):
        return shard_slice(self.grad, lax.rem(t, 16), plane * 2 + lax.div(t, 16))

    def piece_value(self, plane, t):
        rows = pl.ds(pl.multiple_of(lax.rem(t, 16) * PR, 16), PR)
        cols = pl.ds(pl.multiple_of((plane * 2 + lax.div(t, 16)) * PC, PC), PC)
        return self.grad[rows, cols]

    def start_far(self):
        z, i = self.z, self.i
        core = lax.rem(self.s, 2)
        two = lax.rem(z + 2 + 4 * core, PLANES)
        opposite = plane_at(z, 4)

        def go_two(j, _):
            t = lax.rem(i + j, INPLANE)
            send(
                self.piece(opposite, t),
                self.met2.at[core, 64 + lax.div(i, 2)],
                self.out_sem,
                self.sems.at[4 + core],
                device_at(two, t),
            )
            return 0

        def go_one(j, _):
            t = lax.rem(i + j, INPLANE)
            for side in range(2):
                sign = 1 - 2 * side
                send(
                    self.piece(plane_at(z, 3 * sign), t),
                    self.met2.at[side, 32 + i],
                    self.out_sem,
                    self.sems.at[4 + side],
                    device_at(plane_at(z, sign), t),
                )
            return 0

        lax.fori_loop(0, INPLANE, go_two, 0)
        lax.fori_loop(0, INPLANE, go_one, 0)

    def start_inplane(self):
        z, i = self.z, self.i

        def go(level, j):
            t = lax.rem(i + j, INPLANE)
            for side in range(2):
                sign = 1 - 2 * side
                met = self.met2 if level == 2 else self.met1
                send(
                    self.piece(plane_at(z, level * sign), t),
                    met.at[side, i],
                    self.out_sem,
                    self.sems.at[2 * level + side],
                    device_at(z, t),
                )
            return 0

        def go_own(j, _):
            t = lax.rem(i + j, INPLANE)
            send(self.piece(z, t), self.met0.at[i], self.out_sem, self.sems.at[1], device_at(z, t))
            return 0

        lax.fori_loop(1, INPLANE, lambda j, _: go(2, j), 0)
        lax.fori_loop(1, INPLANE, lambda j, _: go(1, j), 0)
        lax.fori_loop(1, INPLANE, go_own, 0)
        for side in range(2):
            sign = 1 - 2 * side
            self.met2[side, i] = self.piece_value(plane_at(z, 2 * sign), i)
            self.met1[side, i] = self.piece_value(plane_at(z, sign), i)
        self.met0[i] = self.piece_value(z, i)
        self.sums[...] = jnp.zeros_like(self.sums)

    def chain(self, value_at, count, side):
        def step(t, _):
            before = self.sums[self.table[PREV_AT + side * FAR + t]]
            self.sums[t] = before + value_at(t).astype(jnp.float32)
            return 0

        lax.fori_loop(0, count, step, 0)

    def summed(self, which, e):
        return self.sums[self.table[LAST_AT + which * EXPERTS + e]]

    def pass_on(self, level, side):
        sign = 1 - 2 * side
        send(
            self.parts[level].at[side],
            self.parts[2 + level].at[side],
            self.part_sems.at[0, level, side],
            self.part_sems.at[1, level, side],
            device_at(plane_at(self.z, sign), self.i),
        )

    def level_two(self, side):
        take(self.met2.at[side, pl.ds(0, FAR - 1)], self.sems.at[4 + side])
        self.chain(lambda t: self.met2[side, t], FAR, side)

        def put(e, _):
            self.parts[0][side, e] = self.summed(side, e).astype(jnp.bfloat16)
            return 0

        lax.fori_loop(0, EXPERTS, put, 0)
        self.pass_on(0, side)

    def level_one(self, side):
        take(self.met1.at[side, pl.ds(0, INPLANE - 1)], self.sems.at[2 + side])
        self.chain(lambda t: self.met1[side, t], INPLANE, 0)
        take(self.parts[2].at[side], self.part_sems.at[1, 0, side])

        def put(e, _):
            value = self.summed(2, e) + self.parts[2][side, e].astype(jnp.float32)
            self.parts[1][side, e] = value.astype(jnp.bfloat16)
            return 0

        lax.fori_loop(0, EXPERTS, put, 0)
        self.pass_on(1, side)

    def level_zero(self):
        take(self.met0.at[pl.ds(0, INPLANE - 1)], self.sems.at[1])
        self.chain(lambda t: self.met0[t], INPLANE, 0)
        for side in range(2):
            take(self.parts[3].at[side], self.part_sems.at[1, 1, side])

        def put(e, _):
            value = self.parts[3][0, e].astype(jnp.float32) + self.parts[3][1, e].astype(jnp.float32)
            self.total[e] = value + self.summed(2, e)
            return 0

        lax.fori_loop(0, EXPERTS, put, 0)

    def finish(self):
        take(self.met2.at[0], self.out_sem)
        take(self.met2.at[0], self.out_sem)
        take(self.met2.at[0], self.out_sem)
        take(self.met2.at[0, pl.ds(0, 5 * 31 + 96 - 3 * FAR)], self.out_sem)
        for level in range(2):
            for side in range(2):
                take(self.parts[level].at[side], self.part_sems.at[0, level, side])


GATHER_SCRATCH = [
    pltpu.VMEM((INPLANE, PR, PC), jnp.bfloat16),
    pltpu.VMEM((2, INPLANE, PR, PC), jnp.bfloat16),
    pltpu.VMEM((2, FAR, PR, PC), jnp.bfloat16),
    pltpu.VMEM((FAR + 1, PR, PC), jnp.float32),
    pltpu.VMEM((2, EXPERTS, PR, PC), jnp.bfloat16),
    pltpu.VMEM((2, EXPERTS, PR, PC), jnp.bfloat16),
    pltpu.VMEM((2, EXPERTS, PR, PC), jnp.bfloat16),
    pltpu.VMEM((2, EXPERTS, PR, PC), jnp.bfloat16),
    pltpu.SemaphoreType.DMA((6,)),
    pltpu.SemaphoreType.DMA((2, 2, 2)),
]


def first_kernel(table, own, grad, weight, total, *scratch):
    n = len(SPREAD_SCRATCH)
    near, far, picks = scratch[0:2], scratch[2:4], scratch[4]
    spread = Spread(table, own, weight, near, far, picks, *scratch[5:n])
    rest = scratch[n:]
    gather = Gather(table, grad, total, *rest[0:4], rest[4:8], *rest[8:])
    gather.start_far()
    spread.start_own()
    gather.start_inplane()
    spread.inplane(own, 0, 0)
    for side in range(2):
        gather.level_two(side)
    for side in range(2):
        spread.wait_near(side)
        spread.forward(side)
    for side in range(2):
        spread.inplane(near[side], 32 + 32 * side, -1 + 2 * side)
    for side in range(2):
        gather.level_one(side)
    for side in range(2):
        spread.wait_far(side)
        spread.outplane(side, 96 + 48 * side)
    for side in range(2):
        spread.inplane(far[side], 192 + 32 * side, -2 + 4 * side)
    gather.level_zero()
    spread.finish()
    gather.finish()


def second_kernel(table, own, weight, *scratch):
    near, far, picks = scratch[0:2], scratch[2:4], scratch[4]
    spread = Spread(table, own, weight, near, far, picks, *scratch[5:])
    spread.start_own()
    spread.inplane(own, 0, 0)
    for side in range(2):
        spread.wait_near(side)
        spread.forward(side)
    for side in range(2):
        spread.inplane(near[side], 32 + 32 * side, -1 + 2 * side)
    for side in range(2):
        spread.wait_far(side)
        spread.outplane(side, 96 + 48 * side)
    for side in range(2):
        spread.inplane(far[side], 192 + 32 * side, -2 + 4 * side)
    spread.finish()


VMEM = pl.BlockSpec(memory_space=pltpu.VMEM)
SMEM = pl.BlockSpec(memory_space=pltpu.SMEM)


def remote_call(kernel, operands, outs, scratch):
    return pl.pallas_call(
        kernel,
        out_shape=outs,
        in_specs=[SMEM] + [VMEM] * (len(operands) - 1),
        out_specs=tuple(VMEM for _ in outs),
        scratch_shapes=scratch,
        compiler_params=pltpu.CompilerParams(has_side_effects=True, vmem_limit_bytes=60 * 2**20),
    )(*operands)


def sum_tables(place, z):
    planes = place.reshape(PLANES, INPLANE)
    around = lax.dynamic_slice(
        jnp.concatenate([planes, planes], 0), (lax.rem(z + 6, PLANES), 0), (5, INPLANE)
    )
    up = jnp.concatenate([around[2], around[1], around[0].reshape(16, 2)[:, 0]])
    down = jnp.concatenate([around[2], around[3], around[4].reshape(16, 2)[:, 1]])
    both = jnp.stack([up, down])
    at = jnp.arange(FAR, dtype=jnp.int32)
    same = both[:, :, None] == both[:, None, :]
    earlier = at[None, :] < at[:, None]
    prev = jnp.max(jnp.where(same & earlier[None], at[None, None, :], -1), axis=2)
    prev = jnp.where(prev < 0, FAR, prev)
    lists = jnp.stack([up, down, jnp.where(at < INPLANE, up, -1)])
    ids = jnp.arange(EXPERTS, dtype=jnp.int32)
    found = lists[:, None, :] == ids[None, :, None]
    last = jnp.max(jnp.where(found, at[None, None, :], -1), axis=2)
    last = jnp.where(last < 0, FAR, last)
    return jnp.concatenate([place, prev.reshape(-1), last.reshape(-1)])


def shards(
    rows_in,
    cotangent,
    gate_prob,
    row_counts,
    old_place,
    new_place,
    rows_next,
    master,
    moment_one,
    moment_two,
):
    row_count = rows_in.shape[0]
    z = lax.div(lax.axis_index("group"), 2)
    live_rows = (jnp.arange(row_count, dtype=jnp.int32) < row_counts[0])[:, None]
    masked_in = jnp.where(live_rows, rows_in, jnp.zeros_like(rows_in))
    masked_out = jnp.where(live_rows, cotangent, jnp.zeros_like(cotangent))
    scaled_out = (gate_prob[:, None] * masked_out.astype(jnp.float32)).astype(jnp.bfloat16)
    slot_grad = lax.dot_general(
        masked_in, scaled_out, (((0,), (0,)), ((), ())), preferred_element_type=jnp.float32
    ).astype(jnp.bfloat16)
    weight_shape = jax.ShapeDtypeStruct((16 * PR, 16 * PC), jnp.bfloat16)
    table = sum_tables(old_place[:, 0], z)
    weight, grad_sum = remote_call(
        first_kernel,
        (table, master.astype(jnp.bfloat16), slot_grad),
        (weight_shape, jax.ShapeDtypeStruct(master.shape, jnp.float32)),
        SPREAD_SCRATCH + GATHER_SCRATCH,
    )
    first_full = beta_one * moment_one.astype(jnp.float32) + (1.0 - beta_one) * grad_sum
    second_full = beta_two * moment_two.astype(jnp.float32) + (1.0 - beta_two) * grad_sum * grad_sum
    new_master = master - learn_rate * (first_full / fix_one) / (
        jnp.sqrt(second_full / fix_two) + adam_eps
    )
    (weight_next,) = remote_call(
        second_kernel,
        (new_place[:, 0], new_master.astype(jnp.bfloat16)),
        (weight_shape,),
        SPREAD_SCRATCH,
    )
    back_prod = lax.dot_general(
        masked_out, weight, (((1,), (1,)), ((), ())), preferred_element_type=jnp.float32
    )
    input_grad = (gate_prob[:, None] * back_prod).astype(jnp.bfloat16)
    gate_grad = jnp.sum(masked_in.astype(jnp.float32) * back_prod, axis=1)
    next_out = jnp.dot(rows_next, weight_next, preferred_element_type=jnp.float32).astype(
        jnp.bfloat16
    )
    return (
        input_grad,
        gate_grad,
        new_master,
        first_full.astype(jnp.bfloat16),
        second_full.astype(jnp.bfloat16),
        next_out,
    )


def solution(mesh):
    in_specs = (
        P(("group", "slot"), None),
        P(("group", "slot"), None),
        P(("group", "slot")),
        P(("group", "slot")),
        P(),
        P(),
        P(("group", "slot"), None),
        P(None, "slot", "group"),
        P(None, "slot", "group"),
        P(None, "slot", "group"),
    )
    out_specs = (
        P(("group", "slot"), None),
        P(("group", "slot")),
        P(None, "slot", "group"),
        P(None, "slot", "group"),
        P(None, "slot", "group"),
        P(("group", "slot"), None),
    )
    return jax.shard_map(shards, mesh=mesh, in_specs=in_specs, out_specs=out_specs, check_vma=False)
```

time: 273 us -> 235 us (0.86)
  Pallas kernels: 0 us -> 207 us
  waiting for transfers between devices: 198 us -> 0 us
  starting transfers between devices: 31.6 us -> 0 us
  local copies, waits for them, and re-layouts: 26.6 us -> 3.56 us
  other arithmetic: 0.68 us -> 9.13 us
    pallas_call x0 -> x2, Pallas kernels: none -> 207 us  [remote_call(): pl.pallas_call(kernel, out_shape=outs, in_specs=[SMEM] + [VMEM] * (len(op...]
    all_to_all x3 -> x0, waiting for transfers between devices: 198 us -> none  [exchange_both(): parts = lax.all_to_all(parts, axis, split_axis=0, concat_axis=0, tiled=True)]
    all_to_all x3 -> x0, starting transfers between devices: 31.6 us -> none  [exchange_both(): parts = lax.all_to_all(parts, axis, split_axis=0, concat_axis=0, tiled=True)]
    transpose x2 -> x0, local copies, waits for them, and re-layouts: 7.9 us -> none  [joined_along(): return jnp.moveaxis(parts, 0, dim).reshape(lengths)]
    convert_element_type x0 -> x2, other arithmetic: none -> 5.89 us  [the longest x1 3.51 us: shards(): new_master.astype(jnp.bfloat16)]
    gather x2 -> x0, local copies, waits for them, and re-layouts: 5.7 us -> none  [to_slots(): picked = shard_in[expert_of].astype(jnp.bfloat16)]
    dot_general x2 -> x0, matrix products: 5.45 us -> none  [the longest x1 2.83 us: shards(): jnp.einsum('egs,sfgd->efd', owner_map, arrived, preferred_element_type=jn...]
    unnamed x28 -> x18, local copies, waits for them, and re-layouts: 7.66 us -> 2.94 us
  transfers between devices with their start and end apart: 3 -> 0, of which waited for: 3 -> 0; matrix products, arithmetic and copies ran while one was open for 9% -> 0% of each run, Pallas kernels for 0% -> 0%
where the time goes in v1:
time: 235 us
  Pallas kernels  207 us (88%)
  matrix products  14 us (6%)
  other arithmetic  9.13 us (4%)
  local copies, waits for them, and re-layouts  3.56 us (2%)
    pallas_call x2, Pallas kernels, remote_call(): pl.pallas_call(kernel, out_shape=outs, in_specs=[SMEM] + [VMEM] * (len(op...  207 us
    dot_general x1, matrix products, shards(): lax.dot_general(masked_out, weight, (((1,), (1,)), ((), ())), preferred_e...  5.38 us
    dot_general x1, matrix products, shards(): lax.dot_general(masked_in, scaled_out, (((0,), (0,)), ((), ())), preferre...  4.83 us

profile of v1, /device:TPU:1, one launch (start us, length us, event | category | flops | bytes accessed | tf_op | source)
XLA Modules:
  0.0 235.1 jit_solution(12085269731107990773)
XLA Ops:
  0.6 0.0 copy-start
  0.6 0.0 copy-start.7
  0.7 0.0 copy-start.5
  1.5 0.5 broadcast.47
  2.0 1.3 reduce.16
  3.3 0.1 reshape_squeeze.9
  3.5 0.1 reshape_squeeze.10
  3.5 0.1 reshape_squeeze.11
  3.6 0.2 slice_reduce_fusion
  3.8 0.1 add_bitcast_fusion
  3.9 0.1 compare_select_fusion.2
  4.0 0.1 select_reduce_fusion
  4.2 0.1 reduce_max.25
  4.3 0.2 select_reduce_fusion.1
  4.5 0.1 reduce_max.23
  4.6 1.4 pad_add_fusion.table
  5.9 2.4 %convert_element_type.39.own = bf16[64,48,128]{2,1,0:T(8,128)(2,1)} convert(f32[64,48,128]{2,1,0:T(8,128)} %param.17) | non-fusion elementwise | flops 393216 | bytes 2359296 | tf_op jit(solution)/shard_map/convert_element_type | solution.py:464
  8.3 0.0 copy-done.7
  8.3 0.0 copy-done.5
  8.3 4.8 %convolution_convert_fusion.grad = bf16[768,2048]{1,0:T(8,128)(2,1)} fusion(f32[512]{0:T(512)S(1)} %copy-done.7, bf16[512,2048]{1,0:T(8,128)(2,1)S(1)} %copy-done.5, pred[512]{0:T(512)(128)(4,1)S(1)} %iota_compare_fusion.2, bf16[512,768]{1,0:T(8,128)(2,1)} %param.10), kind=kOutput, calls=%fused_computation.1 | convolution fusion | flops 1616773120 | bytes 6031872 | tf_op jit(solution)/shard_map/dot_general | solution.py:457
  13.1 0.0 copy-start.6
  13.1 129.4 %shard_map.145 = (bf16[768,2048]{1,0:T(8,128)(2,1)}, f32[64,48,128]{2,1,0:T(8,128)}) custom-call(s32[608]{0:T(1024)} %pad_add_fusion.table, bf16[64,48,128]{2,1,0:T(8,128)(2,1)} %convert_element_type.39.own, bf16[768,2048]{1,0:T(8,128)(2,1)} %convolution_convert_fusion.grad), custom_call_target="tpu_custom_call" | custom-call | tf_op jit(solution)/shard_map/pallas_call | solution.py:408
  142.6 0.0 copy-done.6
  142.6 0.0 copy-start.1
  142.6 0.0 copy-start.2
  142.6 0.0 copy-start.3
  142.6 0.0 copy-start.4
  142.6 5.4 %multiply_reduce_fusion = (f32[512]{0:T(512)}, bf16[512,768]{1,0:T(8,128)(2,1)}) fusion(bf16[512,768]{1,0:T(8,128)(2,1)S(1)} %copy-done.6, pred[512]{0:T(512)(128)(4,1)S(1)} %iota_compare_fusion.2, f32[512]{0:T(512)S(1)} %copy-done.7, bf16[768,2048]{1,0:T(8,128)(2,1)} %get-tuple-element.8, bf16[512,2048]{1,0:T(8,128)(2,1)S(1)} %copy-done.5), kind=kOutput, calls=%fused_computation.10 | convolution fusion | flops 1614020096 | bytes 6820352 | tf_op jit(solution)/shard_map/dot_general | solution.py:479
  148.0 0.0 copy-done.1
  148.0 0.0 copy-done.2
  148.0 0.0 copy-done.3
  148.0 0.0 copy-done.4
  148.0 3.5 %fusion.9 = (bf16[64,48,128]{2,1,0:T(8,128)(2,1)}, f32[64,48,128]{2,1,0:T(8,128)}, bf16[64,48,128]{2,1,0:T(8,128)(2,1)}, bf16[64,48,128]{2,1,0:T(8,128)(2,1)}) fusion(f32[64,48,128]{2,1,0:T(8,128)S(1)} %copy-done.1, f32[64,48,128]{2,1,0:T(8,128)S(1)} %copy-done.2, bf16[64,48,128]{2,1,0:T(8,128)(2,1)S(1)} %copy-done.3, bf16[64,48,128]{2,1,0:T(8,128)(2,1)S(1)} %copy-done.4), kind=kLoop, calls=%fused_computation.41 | loop fusion | flops 6684672 | bytes 8650752 | tf_op jit(solution)/shard_map/convert_element_type | solution.py:475
  151.5 77.4 %shard_map.146 = bf16[768,2048]{1,0:T(8,128)(2,1)} custom-call(s32[256]{0:T(256)} %bitcast.23, bf16[64,48,128]{2,1,0:T(8,128)(2,1)} %get-tuple-element.30.own), custom_call_target="tpu_custom_call" | custom-call | tf_op jit(solution)/shard_map/pallas_call | solution.py:408
  228.9 0.0 copy-done
  228.9 3.7 %fusion = bf16[512,2048]{0,1:T(8,128)(2,1)S(1)} fusion(bf16[768,2048]{1,0:T(8,128)(2,1)} %shard_map.146, bf16[512,768]{1,0:T(8,128)(2,1)S(1)} %copy-done), kind=kOutput, calls=%fused_computation.3 | convolution fusion | flops 1611661312 | bytes 6029312 | tf_op jit(solution)/shard_map/dot_general | solution.py:484
  232.7 2.4 %copy.18 = bf16[512,2048]{1,0:T(8,128)(2,1)} copy(bf16[512,2048]{0,1:T(8,128)(2,1)S(1)} %fusion) | data formatting | bytes 4194304
  (8 shorter events, 0.1 us)
Async XLA Ops:
  0.6 228.3 %copy-start = (bf16[512,768]{1,0:T(8,128)(2,1)S(1)}, bf16[512,768]{1,0:T(8,128)(2,1)}, u32[]{:S(2)}) copy-start(bf16[512,768]{1,0:T(8,128)(2,1)} %param.16) | copy-start | bytes 2359300
  0.6 7.6 %copy-start.7 = (f32[512]{0:T(512)S(1)}, f32[512]{0:T(512)}, u32[]{:S(2)}) copy-start(f32[512]{0:T(512)} %param.12) | copy-start | bytes 6148
  0.7 7.6 %copy-start.5 = (bf16[512,2048]{1,0:T(8,128)(2,1)S(1)}, bf16[512,2048]{1,0:T(8,128)(2,1)}, u32[]{:S(2)}) copy-start(bf16[512,2048]{1,0:T(8,128)(2,1)} %param.11) | copy-start | bytes 6291460
  13.1 129.4 %copy-start.6 = (bf16[512,768]{1,0:T(8,128)(2,1)S(1)}, bf16[512,768]{1,0:T(8,128)(2,1)}, u32[]{:S(2)}) copy-start(bf16[512,768]{1,0:T(8,128)(2,1)} %param.10) | copy-start | bytes 2359300
  142.6 5.4 %copy-start.1 = (f32[64,48,128]{2,1,0:T(8,128)S(1)}, f32[64,48,128]{2,1,0:T(8,128)}, u32[]{:S(2)}) copy-start(f32[64,48,128]{2,1,0:T(8,128)} %param.17) | copy-start | bytes 4718596
  142.6 5.4 %copy-start.2 = (f32[64,48,128]{2,1,0:T(8,128)S(1)}, f32[64,48,128]{2,1,0:T(8,128)}, u32[]{:S(2)}) copy-start(f32[64,48,128]{2,1,0:T(8,128)} %get-tuple-element.9) | copy-start | bytes 4718596
  142.6 5.4 %copy-start.3 = (bf16[64,48,128]{2,1,0:T(8,128)(2,1)S(1)}, bf16[64,48,128]{2,1,0:T(8,128)(2,1)}, u32[]{:S(2)}) copy-start(bf16[64,48,128]{2,1,0:T(8,128)(2,1)} %param.19) | copy-start | bytes 2359300
  142.6 5.4 %copy-start.4 = (bf16[64,48,128]{2,1,0:T(8,128)(2,1)S(1)}, bf16[64,48,128]{2,1,0:T(8,128)(2,1)}, u32[]{:S(2)}) copy-start(bf16[64,48,128]{2,1,0:T(8,128)(2,1)} %param.18) | copy-start | bytes 2359300

commit v2 on v1

--- a/solution.py
+++ b/solution.py
@@ -64,43 +64,71 @@
     pltpu.make_async_copy(ref, ref, sem).wait()
 
 
+CHUNKS = 4
+CE = EXPERTS // CHUNKS
+PEERS = 5 * INPLANE - 1
+
+
+def meet():
+    z, i, _, _ = my_place()
+    barrier = pltpu.get_barrier_semaphore()
+
+    def go(n, _):
+        m = PEERS - n
+        k = lax.div(m, INPLANE)
+        plane = lax.rem(z + k + 3 * lax.div(k, 3), PLANES)
+        g, s = device_at(plane, lax.rem(i + m, INPLANE))
+        pl.semaphore_signal(barrier, inc=1, device_id=(g, s), device_id_type=MESH)
+        return 0
+
+    lax.fori_loop(0, PEERS, go, 0)
+    pl.semaphore_wait(barrier, PEERS)
+
+
 class Spread:
-    def __init__(self, place, own, weight, near, far, picks, ring_sems, out_sem, in_sems):
-        self.place, self.own, self.weight = place, own, weight
-        self.near, self.far, self.picks = near, far, picks
-        self.ring_sems, self.out_sem, self.in_sems = ring_sems, out_sem, in_sems
+    def __init__(self, place, base, own, weight, bufs):
+        self.place, self.base, self.own, self.weight = place, base, own, weight
+        self.near, self.far, self.picks = bufs[0:2], bufs[2:4], bufs[4]
+        self.ring_sems, self.out_sem, self.in_sems = bufs[5:8]
         self.z, self.i, self.g, self.s = my_place()
         self.xlo = lax.rem(self.g, 2)
 
-    def ring(self, src, dst, hop, side):
+    def expert(self, plane, t):
+        return self.place[self.base + plane * INPLANE + t]
+
+    def ring(self, src, dst, hop, side, chunk):
+        part = pl.ds(chunk * CE, CE)
         send(
-            src,
-            dst,
-            self.ring_sems.at[0, hop, side],
-            self.ring_sems.at[1, hop, side],
+            src.at[part],
+            dst.at[part],
+            self.ring_sems.at[0, hop, side, chunk],
+            self.ring_sems.at[1, hop, side, chunk],
             device_at(plane_at(self.z, 1 - 2 * side), self.i),
         )
 
-    def start_own(self):
+    def start_own(self, chunk):
         for side in range(2):
-            self.ring(self.own, self.near[side], 0, side)
-
-    def wait_near(self, side):
-        take(self.near[side], self.ring_sems.at[1, 0, side])
-
-    def forward(self, side):
-        self.ring(self.near[side], self.far[side], 1, side)
-
-    def wait_far(self, side):
-        take(self.far[side], self.ring_sems.at[1, 1, side])
-
-    def inplane(self, ref, base, k):
+            self.ring(self.own, self.near[side], 0, side, chunk)
+
+    def forward(self, chunk):
+        for side in range(2):
+            take(self.near[side].at[pl.ds(chunk * CE, CE)], self.ring_sems.at[1, 0, side, chunk])
+            self.ring(self.near[side], self.far[side], 1, side, chunk)
+
+    def wait_far(self):
+        for chunk in range(CHUNKS):
+            for side in range(2):
+                take(self.far[side].at[pl.ds(chunk * CE, CE)], self.ring_sems.at[1, 1, side, chunk])
+
+    def inplane(self, k):
         z, i = self.z, self.i
+        ref = {0: self.own, -1: self.near[0], 1: self.near[1], -2: self.far[0], 2: self.far[1]}[k]
+        base = {0: 0, -1: 32, 1: 64, -2: 192, 2: 224}[k]
         column = plane_at(z, k) * 2 + self.xlo
 
         def pick(j, _):
             t = lax.rem(i + j, INPLANE)
-            self.picks[base + j] = ref[self.place[z * INPLANE + t]]
+            self.picks[base + j] = ref[self.expert(z, t)]
             return 0
 
         def go(j, _):
@@ -120,60 +148,68 @@
         cols = pl.ds(pl.multiple_of(column * PC, PC), PC)
         self.weight[rows, cols] = self.picks[base]
 
-    def outplane(self, side, base):
-        ref = self.far[side]
+    def other(self, side, j):
+        return lax.rem((lax.div(self.i, 2) + j) * 2, INPLANE) + side
+
+    def pick_out(self, side):
+        ref, base = self.far[side], 96 + 48 * side
         sign = 1 - 2 * side
-        z, i = self.z, self.i
-        column = plane_at(z, -2 * sign) * 2 + self.xlo
-        one, two = plane_at(z, sign), plane_at(z, 2 * sign)
-
-        def other(j):
-            return lax.rem((lax.div(i, 2) + j) * 2, INPLANE) + side
+        one, two = plane_at(self.z, sign), plane_at(self.z, 2 * sign)
+
+        def pick_two(j, _):
+            self.picks[base + 32 + j] = ref[self.expert(two, self.other(side, j))]
+            return 0
 
         def pick_one(j, _):
-            t = lax.rem(i + j, INPLANE)
-            self.picks[base + j] = ref[self.place[one * INPLANE + t]]
-            return 0
-
-        def pick_two(j, _):
-            self.picks[base + 32 + j] = ref[self.place[two * INPLANE + other(j)]]
-            return 0
-
-        def go_one(j, _):
-            t = lax.rem(i + j, INPLANE)
-            send(
-                self.picks.at[base + j],
-                shard_slice(self.weight, self.s, column),
-                self.out_sem,
-                self.in_sems.at[3 - 3 * sign],
-                device_at(one, t),
-            )
-            return 0
-
-        def go_two(j, _):
-            send(
-                self.picks.at[base + 32 + j],
-                shard_slice(self.weight, self.s, column),
-                self.out_sem,
-                self.in_sems.at[7],
-                device_at(two, other(j)),
-            )
+            self.picks[base + j] = ref[self.expert(one, lax.rem(self.i + j, INPLANE))]
             return 0
 
         lax.fori_loop(0, 16, pick_two, 0)
         lax.fori_loop(0, INPLANE, pick_one, 0)
+
+    def out_two(self):
+        def go_two(j, _):
+            for side in range(2):
+                sign = 1 - 2 * side
+                column = plane_at(self.z, -2 * sign) * 2 + self.xlo
+                send(
+                    self.picks.at[96 + 48 * side + 32 + j],
+                    shard_slice(self.weight, self.s, column),
+                    self.out_sem,
+                    self.in_sems.at[7],
+                    device_at(plane_at(self.z, 2 * sign), self.other(side, j)),
+                )
+            return 0
+
         lax.fori_loop(0, 16, go_two, 0)
+
+    def out_one(self):
+        def go_one(j, _):
+            for side in range(2):
+                sign = 1 - 2 * side
+                column = plane_at(self.z, -2 * sign) * 2 + self.xlo
+                send(
+                    self.picks.at[96 + 48 * side + j],
+                    shard_slice(self.weight, self.s, column),
+                    self.out_sem,
+                    self.in_sems.at[3 - 3 * sign],
+                    device_at(plane_at(self.z, sign), lax.rem(self.i + j, INPLANE)),
+                )
+            return 0
+
         lax.fori_loop(0, INPLANE, go_one, 0)
 
-    def finish(self):
-        for k in range(-3, 5):
-            count = 31 if -2 <= k <= 2 else 32
-            take(self.picks.at[pl.ds(0, count)], self.in_sems.at[k + 3])
-        sent = 5 * 31 + 2 * 48
-        take(self.picks.at[pl.ds(0, sent)], self.out_sem)
-        for hop in range(2):
-            for side in range(2):
-                take(self.own, self.ring_sems.at[0, hop, side])
+    def arrived(self, k):
+        count = 31 if -2 <= k <= 2 else 32
+        take(self.picks.at[pl.ds(0, count)], self.in_sems.at[k + 3])
+
+    def sent(self):
+        take(self.picks.at[pl.ds(0, 5 * 31 + 2 * 48)], self.out_sem)
+        for chunk in range(CHUNKS):
+            for hop in range(2):
+                for side in range(2):
+                    part = self.own.at[pl.ds(chunk * CE, CE)]
+                    take(part, self.ring_sems.at[0, hop, side, chunk])
 
 
 SPREAD_SCRATCH = [
@@ -182,15 +218,15 @@
     pltpu.VMEM((EXPERTS, PR, PC), jnp.bfloat16),
     pltpu.VMEM((EXPERTS, PR, PC), jnp.bfloat16),
     pltpu.VMEM((256, PR, PC), jnp.bfloat16),
-    pltpu.SemaphoreType.DMA((2, 2, 2)),
+    pltpu.SemaphoreType.DMA((2, 2, 2, CHUNKS)),
     pltpu.SemaphoreType.DMA,
     pltpu.SemaphoreType.DMA((8,)),
 ]
 
 
 class Gather:
-    def __init__(self, table, grad, total, met0, met1, met2, sums, parts, sems, part_sems):
-        self.table, self.grad, self.total = table, grad, total
+    def __init__(self, table, grad, met0, met1, met2, sums, parts, sems, part_sems):
+        self.table, self.grad = table, grad
         self.met0, self.met1, self.met2 = met0, met1, met2
         self.sums = sums
         self.parts = parts
@@ -322,12 +358,9 @@
         for side in range(2):
             take(self.parts[3].at[side], self.part_sems.at[1, 1, side])
 
-        def put(e, _):
-            value = self.parts[3][0, e].astype(jnp.float32) + self.parts[3][1, e].astype(jnp.float32)
-            self.total[e] = value + self.summed(2, e)
-            return 0
-
-        lax.fori_loop(0, EXPERTS, put, 0)
+    def total(self, e):
+        value = self.parts[3][0, e].astype(jnp.float32) + self.parts[3][1, e].astype(jnp.float32)
+        return value + self.summed(2, e)
 
     def finish(self):
         take(self.met2.at[0], self.out_sem)
@@ -353,66 +386,150 @@
 ]
 
 
-def first_kernel(table, own, grad, weight, total, *scratch):
+STATE = (EXPERTS, PR, PC)
+STATE_SCRATCH = [
+    pltpu.VMEM(STATE, jnp.float32),
+    pltpu.VMEM(STATE, jnp.bfloat16),
+    pltpu.VMEM(STATE, jnp.bfloat16),
+    pltpu.VMEM(STATE, jnp.bfloat16),
+    pltpu.VMEM(STATE, jnp.bfloat16),
+    pltpu.SemaphoreType.DMA((6,)),
+]
+
+
+def step_kernel(
+    table,
+    grad,
+    master_in,
+    first_in,
+    second_in,
+    weight,
+    weight_next,
+    master_out,
+    first_out,
+    second_out,
+    *scratch,
+):
     n = len(SPREAD_SCRATCH)
-    near, far, picks = scratch[0:2], scratch[2:4], scratch[4]
-    spread = Spread(table, own, weight, near, far, picks, *scratch[5:n])
-    rest = scratch[n:]
-    gather = Gather(table, grad, total, *rest[0:4], rest[4:8], *rest[8:])
+    m = len(GATHER_SCRATCH)
+    master, first, second, own, own_next, state_sems = scratch[2 * n + m :]
+    now = Spread(table, 0, own, weight, scratch[0:n])
+    after = Spread(table, TABLE, own_next, weight_next, scratch[n : 2 * n])
+    rest = scratch[2 * n : 2 * n + m]
+    gather = Gather(table, grad, *rest[0:4], rest[4:8], *rest[8:])
+
+    loads = [
+        pltpu.make_async_copy(src, dst, state_sems.at[at])
+        for at, (src, dst) in enumerate(((master_in, master), (first_in, first), (second_in, second)))
+    ]
+    for load in loads:
+        load.start()
+    meet()
+    loads[0].wait()
+
+    def cast(e, _):
+        own[e] = master[e].astype(jnp.bfloat16)
+        return 0
+
+    lax.fori_loop(0, EXPERTS, cast, 0)
     gather.start_far()
-    spread.start_own()
+    for chunk in range(CHUNKS):
+        now.start_own(chunk)
     gather.start_inplane()
-    spread.inplane(own, 0, 0)
+    now.inplane(0)
+    now.forward(0)
+    now.forward(1)
     for side in range(2):
         gather.level_two(side)
-    for side in range(2):
-        spread.wait_near(side)
-        spread.forward(side)
-    for side in range(2):
-        spread.inplane(near[side], 32 + 32 * side, -1 + 2 * side)
+    now.forward(2)
+    now.forward(3)
+    now.inplane(-1)
+    now.inplane(1)
     for side in range(2):
         gather.level_one(side)
+    now.wait_far()
     for side in range(2):
-        spread.wait_far(side)
-        spread.outplane(side, 96 + 48 * side)
+        now.pick_out(side)
+    now.out_two()
+    now.inplane(-2)
+    now.inplane(2)
+    gather.level_zero()
+    for load in loads[1:]:
+        load.wait()
+
+    def update(e, _):
+        grad_sum = gather.total(e)
+        first_full = beta_one * first[e].astype(jnp.float32) + (1.0 - beta_one) * grad_sum
+        second_full = (
+            beta_two * second[e].astype(jnp.float32) + (1.0 - beta_two) * grad_sum * grad_sum
+        )
+        moved = master[e] - learn_rate * (first_full / fix_one) / (
+            jnp.sqrt(second_full / fix_two) + adam_eps
+        )
+        master[e] = moved
+        own_next[e] = moved.astype(jnp.bfloat16)
+        first[e] = first_full.astype(jnp.bfloat16)
+        second[e] = second_full.astype(jnp.bfloat16)
+        return 0
+
+    for chunk in range(CHUNKS):
+        lax.fori_loop(chunk * CE, (chunk + 1) * CE, update, 0)
+        after.start_own(chunk)
+    stores = [
+        pltpu.make_async_copy(src, dst, state_sems.at[3 + at])
+        for at, (src, dst) in enumerate(
+            ((master, master_out), (first, first_out), (second, second_out))
+        )
+    ]
+    for store in stores:
+        store.start()
+    after.inplane(0)
+    for chunk in range(CHUNKS):
+        after.forward(chunk)
+    now.out_one()
+    after.inplane(-1)
+    after.inplane(1)
+    after.wait_far()
     for side in range(2):
-        spread.inplane(far[side], 192 + 32 * side, -2 + 4 * side)
-    gather.level_zero()
-    spread.finish()
+        after.pick_out(side)
+    after.out_two()
+    after.out_one()
+    after.inplane(-2)
+    after.inplane(2)
+    for k in range(-3, 5):
+        now.arrived(k)
+    for store in stores:
+        store.wait()
+    now.sent()
     gather.finish()
-
-
-def second_kernel(table, own, weight, *scratch):
-    near, far, picks = scratch[0:2], scratch[2:4], scratch[4]
-    spread = Spread(table, own, weight, near, far, picks, *scratch[5:])
-    spread.start_own()
-    spread.inplane(own, 0, 0)
-    for side in range(2):
-        spread.wait_near(side)
-        spread.forward(side)
-    for side in range(2):
-        spread.inplane(near[side], 32 + 32 * side, -1 + 2 * side)
-    for side in range(2):
-        spread.wait_far(side)
-        spread.outplane(side, 96 + 48 * side)
-    for side in range(2):
-        spread.inplane(far[side], 192 + 32 * side, -2 + 4 * side)
-    spread.finish()
-
-
+    for k in range(-3, 5):
+        after.arrived(k)
+    after.sent()
+
+
+ANY = pl.BlockSpec(memory_space=pl.ANY)
 VMEM = pl.BlockSpec(memory_space=pltpu.VMEM)
 SMEM = pl.BlockSpec(memory_space=pltpu.SMEM)
 
 
-def remote_call(kernel, operands, outs, scratch):
+def step_call(table, grad, master, moment_one, moment_two):
+    weight = jax.ShapeDtypeStruct((16 * PR, 16 * PC), jnp.bfloat16)
     return pl.pallas_call(
-        kernel,
-        out_shape=outs,
-        in_specs=[SMEM] + [VMEM] * (len(operands) - 1),
-        out_specs=tuple(VMEM for _ in outs),
-        scratch_shapes=scratch,
-        compiler_params=pltpu.CompilerParams(has_side_effects=True, vmem_limit_bytes=60 * 2**20),
-    )(*operands)
+        step_kernel,
+        out_shape=(
+            weight,
+            weight,
+            jax.ShapeDtypeStruct(STATE, jnp.float32),
+            jax.ShapeDtypeStruct(STATE, jnp.bfloat16),
+            jax.ShapeDtypeStruct(STATE, jnp.bfloat16),
+        ),
+        in_specs=[SMEM, VMEM, ANY, ANY, ANY],
+        out_specs=(VMEM, VMEM, ANY, ANY, ANY),
+        scratch_shapes=SPREAD_SCRATCH * 2 + GATHER_SCRATCH + STATE_SCRATCH,
+        compiler_params=pltpu.CompilerParams(
+            has_side_effects=True, collective_id=0, vmem_limit_bytes=60 * 2**20
+        ),
+    )(table, grad, master, moment_one, moment_two)
 
 
 def sum_tables(place, z):
@@ -433,7 +550,7 @@
     found = lists[:, None, :] == ids[None, :, None]
     last = jnp.max(jnp.where(found, at[None, None, :], -1), axis=2)
     last = jnp.where(last < 0, FAR, last)
-    return jnp.concatenate([place, prev.reshape(-1), last.reshape(-1)])
+    return prev.reshape(-1), last.reshape(-1)
 
 
 def shards(
@@ -457,24 +574,10 @@
     slot_grad = lax.dot_general(
         masked_in, scaled_out, (((0,), (0,)), ((), ())), preferred_element_type=jnp.float32
     ).astype(jnp.bfloat16)
-    weight_shape = jax.ShapeDtypeStruct((16 * PR, 16 * PC), jnp.bfloat16)
-    table = sum_tables(old_place[:, 0], z)
-    weight, grad_sum = remote_call(
-        first_kernel,
-        (table, master.astype(jnp.bfloat16), slot_grad),
-        (weight_shape, jax.ShapeDtypeStruct(master.shape, jnp.float32)),
-        SPREAD_SCRATCH + GATHER_SCRATCH,
-    )
-    first_full = beta_one * moment_one.astype(jnp.float32) + (1.0 - beta_one) * grad_sum
-    second_full = beta_two * moment_two.astype(jnp.float32) + (1.0 - beta_two) * grad_sum * grad_sum
-    new_master = master - learn_rate * (first_full / fix_one) / (
-        jnp.sqrt(second_full / fix_two) + adam_eps
-    )
-    (weight_next,) = remote_call(
-        second_kernel,
-        (new_place[:, 0], new_master.astype(jnp.bfloat16)),
-        (weight_shape,),
-        SPREAD_SCRATCH,
+    old, new = old_place.reshape(-1), new_place.reshape(-1)
+    table = jnp.concatenate([old, *sum_tables(old, z), new])
+    weight, weight_next, new_master, new_first, new_second = step_call(
+        table, slot_grad, master, moment_one, moment_two
     )
     back_prod = lax.dot_general(
         masked_out, weight, (((1,), (1,)), ((), ())), preferred_element_type=jnp.float32
@@ -488,8 +591,8 @@
         input_grad,
         gate_grad,
         new_master,
-        first_full.astype(jnp.bfloat16),
-        second_full.astype(jnp.bfloat16),
+        new_first,
+        new_second,
         next_out,
     )
 

time: 235 us -> 205 us (0.87)
  Pallas kernels: 207 us -> 179 us
  other arithmetic: 9.13 us -> 3.26 us
  local copies, waits for them, and re-layouts: 3.56 us -> 8.08 us
    pallas_call x2 -> x1, Pallas kernels: 207 us -> 179 us  [step_call(): pl.pallas_call(step_kernel, out_shape=(weight, weight, jax.ShapeDtypeStru...]
    convert_element_type x2 -> x0, other arithmetic: 5.89 us -> none  [the longest x1 3.51 us: shards(): new_master.astype(jnp.bfloat16)]
    unnamed x18 -> x19, local copies, waits for them, and re-layouts: 2.94 us -> 7.45 us
where the time goes in v2:
time: 205 us
  Pallas kernels  179 us (87%)
  matrix products  12.8 us (6%)
  local copies, waits for them, and re-layouts  8.08 us (4%)
  other arithmetic  3.26 us (2%)
    pallas_call x1, Pallas kernels, step_call(): pl.pallas_call(step_kernel, out_shape=(weight, weight, jax.ShapeDtypeStru...  179 us
    unnamed x19, local copies, waits for them, and re-layouts  7.45 us
    dot_general x1, matrix products, shards(): lax.dot_general(masked_in, scaled_out, (((0,), (0,)), ((), ())), preferre...  5.55 us
    dot_general x1, matrix products, shards(): lax.dot_general(masked_out, weight, (((1,), (1,)), ((), ())), preferred_e...  5.38 us

profile of v2, /device:TPU:1, one launch (start us, length us, event | category | flops | bytes accessed | tf_op | source)
XLA Modules:
  0.0 204.7 jit_solution(14419272860759987332)
XLA Ops:
  0.6 0.0 copy-start
  1.4 0.5 broadcast.44
  1.9 1.3 reduce.16
  3.2 0.1 reshape_reshape.3
  3.4 0.1 reshape_squeeze.6
  3.4 0.1 reshape_squeeze.7
  3.5 0.2 slice_reduce_fusion
  3.7 0.1 add_bitcast_fusion
  3.8 0.1 compare_select_fusion.2
  3.9 0.1 select_reduce_fusion
  4.1 0.1 reduce_max.25
  4.2 0.2 select_reduce_fusion.1
  4.4 0.1 reduce_max.23
  4.5 1.4 pad_add_fusion.table
  5.8 5.5 %convolution_convert_fusion.grad = bf16[768,2048]{1,0:T(8,128)(2,1)} fusion(f32[512]{0:T(512)} %param.12, bf16[512,2048]{1,0:T(8,128)(2,1)} %param.11, pred[512]{0:T(512)(128)(4,1)S(1)} %iota_compare_fusion.2, bf16[512,768]{1,0:T(8,128)(2,1)} %param.10), kind=kOutput, calls=%fused_computation.1 | convolution fusion | flops 1616773120 | bytes 6031872 | tf_op jit(solution)/shard_map/dot_general | solution.py:574
  11.4 0.0 copy-start.4
  11.4 0.0 copy-start.5
  11.4 0.0 copy-start.6
  11.4 179.1 %shard_map.145 = (bf16[768,2048]{1,0:T(8,128)(2,1)}, bf16[768,2048]{1,0:T(8,128)(2,1)}, f32[64,48,128]{2,1,0:T(8,128)}, bf16[64,48,128]{2,1,0:T(8,128)(2,1)}, bf16[64,48,128]{2,1,0:T(8,128)(2,1)}) custom-call(s32[864]{0:T(1024)} %pad_add_fusion.table, bf16[768,2048]{1,0:T(8,128)(2,1)} %convolution_convert_fusion.grad, f32[64,48,128]{2,1,0:T(8,128)} %master_in.1, ...), custom_call_target="tpu_custom_call" | custom-call | tf_op jit(solution)/shard_map/pallas_call | solution.py:517
  190.4 0.0 copy-done.4
  190.4 0.0 copy-done.5
  190.5 0.0 copy-done.6
  190.5 0.0 copy-start.3
  190.5 5.4 %multiply_reduce_fusion = (f32[512]{0:T(512)}, bf16[512,768]{1,0:T(8,128)(2,1)}) fusion(bf16[512,768]{1,0:T(8,128)(2,1)S(1)} %copy-done.5, pred[512]{0:T(512)(128)(4,1)S(1)} %iota_compare_fusion.2, f32[512]{0:T(512)S(1)} %copy-done.6, bf16[768,2048]{1,0:T(8,128)(2,1)} %get-tuple-element.11, bf16[512,2048]{1,0:T(8,128)(2,1)S(1)} %copy-done.4), kind=kOutput, calls=%fused_computation.6 | convolution fusion | flops 1614020096 | bytes 6820352 | tf_op jit(solution)/shard_map/dot_general | solution.py:582
  195.9 0.0 copy-done
  195.9 0.0 copy-done.3
  195.9 1.9 fusion
  197.7 2.4 %copy.18 = bf16[512,2048]{1,0:T(8,128)(2,1)} copy(bf16[512,2048]{0,1:T(8,128)(2,1)S(1)} %fusion) | data formatting | bytes 4194304
  200.1 0.0 copy-start.2
  200.1 0.0 copy-start.1
  200.1 2.8 %copy.23 = f32[64,48,128]{2,1,0:T(8,128)} copy(f32[64,48,128]{2,1,0:T(8,128)} %get-tuple-element.57) | data formatting | bytes 3145728
  202.9 0.0 copy-done.2
  202.9 0.9 copy.24
  203.8 0.0 copy-done.1
  203.8 0.9 copy.25
  (8 shorter events, 0.1 us)
Async XLA Ops:
  0.6 195.2 %copy-start = (bf16[512,768]{1,0:T(8,128)(2,1)S(1)}, bf16[512,768]{1,0:T(8,128)(2,1)}, u32[]{:S(2)}) copy-start(bf16[512,768]{1,0:T(8,128)(2,1)} %param.16) | copy-start | bytes 2359300
  11.4 179.1 %copy-start.4 = (bf16[512,2048]{1,0:T(8,128)(2,1)S(1)}, bf16[512,2048]{1,0:T(8,128)(2,1)}, u32[]{:S(2)}) copy-start(bf16[512,2048]{1,0:T(8,128)(2,1)} %param.11) | copy-start | bytes 6291460
  11.4 179.1 %copy-start.5 = (bf16[512,768]{1,0:T(8,128)(2,1)S(1)}, bf16[512,768]{1,0:T(8,128)(2,1)}, u32[]{:S(2)}) copy-start(bf16[512,768]{1,0:T(8,128)(2,1)} %param.10) | copy-start | bytes 2359300
  11.4 179.1 %copy-start.6 = (f32[512]{0:T(512)S(1)}, f32[512]{0:T(512)}, u32[]{:S(2)}) copy-start(f32[512]{0:T(512)} %param.12) | copy-start | bytes 6148
  190.5 5.4 %copy-start.3 = (bf16[768,2048]{1,0:T(8,128)(2,1)S(1)}, bf16[768,2048]{1,0:T(8,128)(2,1)}, u32[]{:S(2)}) copy-start(bf16[768,2048]{1,0:T(8,128)(2,1)} %get-tuple-element.15) | copy-start | bytes 9437188
  200.1 2.8 %copy-start.2 = (bf16[64,48,128]{2,1,0:T(8,128)(2,1)S(1)}, bf16[64,48,128]{2,1,0:T(8,128)(2,1)}, u32[]{:S(2)}) copy-start(bf16[64,48,128]{2,1,0:T(8,128)(2,1)} %get-tuple-element.58) | copy-start | bytes 2359300
  200.1 3.7 %copy-start.1 = (bf16[64,48,128]{2,1,0:T(8,128)(2,1)S(1)}, bf16[64,48,128]{2,1,0:T(8,128)(2,1)}, u32[]{:S(2)}) copy-start(bf16[64,48,128]{2,1,0:T(8,128)(2,1)} %get-tuple-element.59) | copy-start | bytes 2359300

commit v3 on v2

--- a/solution.py
+++ b/solution.py
@@ -1,5 +1,3 @@
-import functools
-
 import jax
 import jax.numpy as jnp
 from jax import lax
@@ -21,10 +19,6 @@
 INPLANE = 32
 FAR = 80
 MESH = pl.DeviceIdType.MESH
-
-PREV_AT = 256
-LAST_AT = PREV_AT + 2 * FAR
-TABLE = LAST_AT + 3 * EXPERTS
 
 
 def my_place():
@@ -65,7 +59,7 @@
 
 
 CHUNKS = 4
-CE = EXPERTS // CHUNKS
+PARTS = ((0, 32), (32, 16))
 PEERS = 5 * INPLANE - 1
 
 
@@ -82,22 +76,24 @@
         return 0
 
     lax.fori_loop(0, PEERS, go, 0)
-    pl.semaphore_wait(barrier, PEERS)
+    return barrier
 
 
 class Spread:
-    def __init__(self, place, base, own, weight, bufs):
-        self.place, self.base, self.own, self.weight = place, base, own, weight
+    def __init__(self, place, own, weight, first_row, chunks, bufs):
+        self.place, self.own, self.weight = place, own, weight
+        self.first_row, self.count = first_row, own.shape[1]
+        self.chunks, self.step = chunks, EXPERTS // chunks
         self.near, self.far, self.picks = bufs[0:2], bufs[2:4], bufs[4]
         self.ring_sems, self.out_sem, self.in_sems = bufs[5:8]
         self.z, self.i, self.g, self.s = my_place()
         self.xlo = lax.rem(self.g, 2)
 
     def expert(self, plane, t):
-        return self.place[self.base + plane * INPLANE + t]
+        return self.place[plane * INPLANE + t]
 
     def ring(self, src, dst, hop, side, chunk):
-        part = pl.ds(chunk * CE, CE)
+        part = pl.ds(chunk * self.step, self.step)
         send(
             src.at[part],
             dst.at[part],
@@ -112,13 +108,21 @@
 
     def forward(self, chunk):
         for side in range(2):
-            take(self.near[side].at[pl.ds(chunk * CE, CE)], self.ring_sems.at[1, 0, side, chunk])
+            part = self.near[side].at[pl.ds(chunk * self.step, self.step)]
+            take(part, self.ring_sems.at[1, 0, side, chunk])
             self.ring(self.near[side], self.far[side], 1, side, chunk)
 
     def wait_far(self):
-        for chunk in range(CHUNKS):
+        for chunk in range(self.chunks):
             for side in range(2):
-                take(self.far[side].at[pl.ds(chunk * CE, CE)], self.ring_sems.at[1, 1, side, chunk])
+                part = self.far[side].at[pl.ds(chunk * self.step, self.step)]
+                take(part, self.ring_sems.at[1, 1, side, chunk])
+
+    def span(self):
+        return pl.ds(pl.multiple_of(self.s * PR + self.first_row, 16), self.count)
+
+    def target(self, column):
+        return self.weight.at[self.span(), pl.ds(pl.multiple_of(column * PC, PC), PC)]
 
     def inplane(self, k):
         z, i = self.z, self.i
@@ -135,7 +139,7 @@
             t = lax.rem(i + j, INPLANE)
             send(
                 self.picks.at[base + j],
-                shard_slice(self.weight, self.s, column),
+                self.target(column),
                 self.out_sem,
                 self.in_sems.at[k + 3],
                 device_at(z, t),
@@ -144,9 +148,7 @@
 
         lax.fori_loop(0, INPLANE, pick, 0)
         lax.fori_loop(1, INPLANE, go, 0)
-        rows = pl.ds(pl.multiple_of(self.s * PR, 16), PR)
-        cols = pl.ds(pl.multiple_of(column * PC, PC), PC)
-        self.weight[rows, cols] = self.picks[base]
+        self.weight[self.span(), pl.ds(pl.multiple_of(column * PC, PC), PC)] = self.picks[base]
 
     def other(self, side, j):
         return lax.rem((lax.div(self.i, 2) + j) * 2, INPLANE) + side
@@ -174,7 +176,7 @@
                 column = plane_at(self.z, -2 * sign) * 2 + self.xlo
                 send(
                     self.picks.at[96 + 48 * side + 32 + j],
-                    shard_slice(self.weight, self.s, column),
+                    self.target(column),
                     self.out_sem,
                     self.in_sems.at[7],
                     device_at(plane_at(self.z, 2 * sign), self.other(side, j)),
@@ -190,7 +192,7 @@
                 column = plane_at(self.z, -2 * sign) * 2 + self.xlo
                 send(
                     self.picks.at[96 + 48 * side + j],
-                    shard_slice(self.weight, self.s, column),
+                    self.target(column),
                     self.out_sem,
                     self.in_sems.at[3 - 3 * sign],
                     device_at(plane_at(self.z, sign), lax.rem(self.i + j, INPLANE)),
@@ -205,28 +207,26 @@
 
     def sent(self):
         take(self.picks.at[pl.ds(0, 5 * 31 + 2 * 48)], self.out_sem)
-        for chunk in range(CHUNKS):
+        for chunk in range(self.chunks):
             for hop in range(2):
                 for side in range(2):
-                    part = self.own.at[pl.ds(chunk * CE, CE)]
+                    part = self.own.at[pl.ds(chunk * self.step, self.step)]
                     take(part, self.ring_sems.at[0, hop, side, chunk])
 
 
-SPREAD_SCRATCH = [
-    pltpu.VMEM((EXPERTS, PR, PC), jnp.bfloat16),
-    pltpu.VMEM((EXPERTS, PR, PC), jnp.bfloat16),
-    pltpu.VMEM((EXPERTS, PR, PC), jnp.bfloat16),
-    pltpu.VMEM((EXPERTS, PR, PC), jnp.bfloat16),
-    pltpu.VMEM((256, PR, PC), jnp.bfloat16),
-    pltpu.SemaphoreType.DMA((2, 2, 2, CHUNKS)),
-    pltpu.SemaphoreType.DMA,
-    pltpu.SemaphoreType.DMA((8,)),
-]
+def spread_scratch(rows, chunks):
+    shards = [pltpu.VMEM((EXPERTS, rows, PC), jnp.bfloat16) for _ in range(4)]
+    return shards + [
+        pltpu.VMEM((256, rows, PC), jnp.bfloat16),
+        pltpu.SemaphoreType.DMA((2, 2, 2, chunks)),
+        pltpu.SemaphoreType.DMA,
+        pltpu.SemaphoreType.DMA((8,)),
+    ]
 
 
 class Gather:
-    def __init__(self, table, grad, met0, met1, met2, sums, parts, sems, part_sems):
-        self.table, self.grad = table, grad
+    def __init__(self, prev, last, grad, met0, met1, met2, sums, parts, sems, part_sems):
+        self.prev, self.last, self.grad = prev, last, grad
         self.met0, self.met1, self.met2 = met0, met1, met2
         self.sums = sums
         self.parts = parts
@@ -275,7 +275,7 @@
         lax.fori_loop(0, INPLANE, go_two, 0)
         lax.fori_loop(0, INPLANE, go_one, 0)
 
-    def start_inplane(self):
+    def start_inplane(self, level):
         z, i = self.z, self.i
 
         def go(level, j):
@@ -297,26 +297,28 @@
             send(self.piece(z, t), self.met0.at[i], self.out_sem, self.sems.at[1], device_at(z, t))
             return 0
 
-        lax.fori_loop(1, INPLANE, lambda j, _: go(2, j), 0)
-        lax.fori_loop(1, INPLANE, lambda j, _: go(1, j), 0)
-        lax.fori_loop(1, INPLANE, go_own, 0)
+        if level == 0:
+            lax.fori_loop(1, INPLANE, go_own, 0)
+            self.met0[i] = self.piece_value(z, i)
+            return
+        lax.fori_loop(1, INPLANE, lambda j, _: go(level, j), 0)
+        met = self.met2 if level == 2 else self.met1
         for side in range(2):
-            sign = 1 - 2 * side
-            self.met2[side, i] = self.piece_value(plane_at(z, 2 * sign), i)
-            self.met1[side, i] = self.piece_value(plane_at(z, sign), i)
-        self.met0[i] = self.piece_value(z, i)
-        self.sums[...] = jnp.zeros_like(self.sums)
+            met[side, i] = self.piece_value(plane_at(z, level * (1 - 2 * side)), i)
 
     def chain(self, value_at, count, side):
         def step(t, _):
-            before = self.sums[self.table[PREV_AT + side * FAR + t]]
+            before = self.sums[self.prev[side * FAR + t]]
             self.sums[t] = before + value_at(t).astype(jnp.float32)
             return 0
 
         lax.fori_loop(0, count, step, 0)
 
     def summed(self, which, e):
-        return self.sums[self.table[LAST_AT + which * EXPERTS + e]]
+        return self.sums[self.last[which * EXPERTS + e]]
+
+    def clear(self):
+        self.sums[...] = jnp.zeros_like(self.sums)
 
     def pass_on(self, level, side):
         sign = 1 - 2 * side
@@ -358,9 +360,10 @@
         for side in range(2):
             take(self.parts[3].at[side], self.part_sems.at[1, 1, side])
 
-    def total(self, e):
-        value = self.parts[3][0, e].astype(jnp.float32) + self.parts[3][1, e].astype(jnp.float32)
-        return value + self.summed(2, e)
+    def total(self, e, rows):
+        value = self.parts[3][0, e, rows].astype(jnp.float32)
+        value = value + self.parts[3][1, e, rows].astype(jnp.float32)
+        return value + self.sums[self.last[2 * EXPERTS + e], rows]
 
     def finish(self):
         take(self.met2.at[0], self.out_sem)
@@ -387,44 +390,72 @@
 
 
 STATE = (EXPERTS, PR, PC)
-STATE_SCRATCH = [
-    pltpu.VMEM(STATE, jnp.float32),
+ROWS = 512
+FF = 16 * PR
+D = 16 * PC
+BLOCK = 128
+WIDE = 2 * PC
+LOCAL_SCRATCH = [
     pltpu.VMEM(STATE, jnp.bfloat16),
-    pltpu.VMEM(STATE, jnp.bfloat16),
-    pltpu.VMEM(STATE, jnp.bfloat16),
-    pltpu.VMEM(STATE, jnp.bfloat16),
-    pltpu.SemaphoreType.DMA((6,)),
+    *[pltpu.VMEM((EXPERTS, rows, PC), jnp.bfloat16) for _, rows in PARTS],
+    pltpu.VMEM((FF, D), jnp.bfloat16),
+    pltpu.VMEM((FF, D), jnp.bfloat16),
+    pltpu.VMEM((ROWS, FF), jnp.bfloat16),
+    pltpu.VMEM((FF, ROWS), jnp.bfloat16),
+    pltpu.VMEM((ROWS, D), jnp.bfloat16),
+    pltpu.VMEM((ROWS, D), jnp.bfloat16),
+    pltpu.VMEM((ROWS, BLOCK), jnp.float32),
+    pltpu.SemaphoreType.DMA((5,)),
 ]
 
 
+SCRATCHES = [spread_scratch(PR, CHUNKS)] + [spread_scratch(rows, 1) for _, rows in PARTS]
+
 def step_kernel(
-    table,
-    grad,
+    old,
+    new,
+    prev,
+    last,
+    count,
+    gate_in,
+    rows_in,
+    cot_in,
     master_in,
     first_in,
     second_in,
-    weight,
     weight_next,
-    master_out,
-    first_out,
-    second_out,
+    master,
+    first,
+    second,
+    input_grad,
+    gate_grad,
     *scratch,
 ):
-    n = len(SPREAD_SCRATCH)
+    n = len(SCRATCHES[0])
     m = len(GATHER_SCRATCH)
-    master, first, second, own, own_next, state_sems = scratch[2 * n + m :]
-    now = Spread(table, 0, own, weight, scratch[0:n])
-    after = Spread(table, TABLE, own_next, weight_next, scratch[n : 2 * n])
-    rest = scratch[2 * n : 2 * n + m]
-    gather = Gather(table, grad, *rest[0:4], rest[4:8], *rest[8:])
-
+    own, own_a, own_b, grad, weight, rows, rows_t, cot, scaled, gate, load_sems = scratch[3 * n + m :]
+    now = Spread(old, own, weight, 0, CHUNKS, scratch[0:n])
+    after = [
+        Spread(new, part, weight_next, PARTS[at][0], 1, scratch[(at + 1) * n : (at + 2) * n])
+        for at, part in enumerate((own_a, own_b))
+    ]
+    rest = scratch[3 * n : 3 * n + m]
+    gather = Gather(prev, last, grad, *rest[0:4], rest[4:8], *rest[8:])
+    z = now.z
+
+    pairs = (
+        (master_in, master),
+        (rows_in, rows),
+        (cot_in, cot),
+        (first_in, first),
+        (second_in, second),
+    )
     loads = [
-        pltpu.make_async_copy(src, dst, state_sems.at[at])
-        for at, (src, dst) in enumerate(((master_in, master), (first_in, first), (second_in, second)))
+        pltpu.make_async_copy(src, dst, load_sems.at[at]) for at, (src, dst) in enumerate(pairs)
     ]
     for load in loads:
         load.start()
-    meet()
+    barrier = meet()
     loads[0].wait()
 
     def cast(e, _):
@@ -432,15 +463,56 @@
         return 0
 
     lax.fori_loop(0, EXPERTS, cast, 0)
-    gather.start_far()
+    pl.semaphore_wait(barrier, PEERS)
     for chunk in range(CHUNKS):
         now.start_own(chunk)
-    gather.start_inplane()
+
     now.inplane(0)
+    loads[1].wait()
+    loads[2].wait()
+    live_count = count[0]
+    for block in range(ROWS // BLOCK):
+        at = pl.ds(block * BLOCK, BLOCK)
+        live = lax.broadcasted_iota(jnp.int32, (BLOCK, BLOCK), 0) + block * BLOCK < live_count
+        factor = jnp.transpose(jnp.broadcast_to(gate_in[block : block + 1, :], (BLOCK, BLOCK)))
+        gate[at, :] = factor
+
+        def mask_rows(c, _, at=at, live=live):
+            cols = pl.ds(pl.multiple_of(c * BLOCK, BLOCK), BLOCK)
+            value = jnp.where(live, rows[at, cols].astype(jnp.float32), 0.0)
+            rows[at, cols] = value.astype(jnp.bfloat16)
+            rows_t[cols, at] = jnp.transpose(value).astype(jnp.bfloat16)
+            return 0
+
+        def mask_cot(c, _, at=at, live=live, factor=factor):
+            cols = pl.ds(pl.multiple_of(c * BLOCK, BLOCK), BLOCK)
+            value = jnp.where(live, cot[at, cols].astype(jnp.float32), 0.0)
+            cot[at, cols] = value.astype(jnp.bfloat16)
+            scaled[at, cols] = (factor * value).astype(jnp.bfloat16)
+            return 0
+
+        lax.fori_loop(0, FF // BLOCK, mask_rows, 0)
+        lax.fori_loop(0, D // BLOCK, mask_cot, 0)
+
+    def slot_grad(p, _):
+        half = lax.div(p + 1, 2)
+        plane = lax.rem(z + 4 + (1 - 2 * lax.rem(p, 2)) * half, PLANES)
+        cols = pl.ds(pl.multiple_of(plane * WIDE, WIDE), WIDE)
+        grad[:, cols] = jnp.dot(
+            rows_t[...], scaled[:, cols], preferred_element_type=jnp.float32
+        ).astype(jnp.bfloat16)
+        return 0
+
+    lax.fori_loop(0, PLANES, slot_grad, 0)
+    gather.clear()
+    gather.start_far()
+    gather.start_inplane(2)
     now.forward(0)
     now.forward(1)
     for side in range(2):
         gather.level_two(side)
+    gather.start_inplane(1)
+    gather.start_inplane(0)
     now.forward(2)
     now.forward(3)
     now.inplane(-1)
@@ -454,82 +526,161 @@
     now.inplane(-2)
     now.inplane(2)
     gather.level_zero()
-    for load in loads[1:]:
+    for load in loads[3:]:
         load.wait()
 
-    def update(e, _):
-        grad_sum = gather.total(e)
-        first_full = beta_one * first[e].astype(jnp.float32) + (1.0 - beta_one) * grad_sum
+    def update(e, rows, own_next):
+        grad_sum = gather.total(e, rows)
+        first_full = beta_one * first[e, rows].astype(jnp.float32) + (1.0 - beta_one) * grad_sum
         second_full = (
-            beta_two * second[e].astype(jnp.float32) + (1.0 - beta_two) * grad_sum * grad_sum
+            beta_two * second[e, rows].astype(jnp.float32)
+            + (1.0 - beta_two) * grad_sum * grad_sum
         )
-        moved = master[e] - learn_rate * (first_full / fix_one) / (
+        moved = master[e, rows] - learn_rate * (first_full / fix_one) / (
             jnp.sqrt(second_full / fix_two) + adam_eps
         )
-        master[e] = moved
+        master[e, rows] = moved
         own_next[e] = moved.astype(jnp.bfloat16)
-        first[e] = first_full.astype(jnp.bfloat16)
-        second[e] = second_full.astype(jnp.bfloat16)
+        first[e, rows] = first_full.astype(jnp.bfloat16)
+        second[e, rows] = second_full.astype(jnp.bfloat16)
         return 0
 
-    for chunk in range(CHUNKS):
-        lax.fori_loop(chunk * CE, (chunk + 1) * CE, update, 0)
-        after.start_own(chunk)
-    stores = [
-        pltpu.make_async_copy(src, dst, state_sems.at[3 + at])
-        for at, (src, dst) in enumerate(
-            ((master, master_out), (first, first_out), (second, second_out))
+    for at, part in enumerate(after):
+        rows_at = pl.ds(*PARTS[at])
+        lax.fori_loop(
+            0, EXPERTS, lambda e, _, rows_at=rows_at, part=part: update(e, rows_at, part.own), 0
         )
-    ]
+        part.start_own(0)
+    for part in after:
+        part.inplane(0)
+    for part in after:
+        part.forward(0)
+        part.inplane(-1)
+        part.inplane(1)
+    now.out_one()
+    for part in after:
+        part.wait_far()
+        for side in range(2):
+            part.pick_out(side)
+        part.inplane(-2)
+        part.inplane(2)
+        part.out_two()
+        part.out_one()
+    for k in range(-3, 5):
+        now.arrived(k)
+
+    def back(block, _):
+        at = pl.ds(pl.multiple_of(block * BLOCK, BLOCK), BLOCK)
+        prod = lax.dot_general(
+            cot[at, :], weight[...], (((1,), (1,)), ((), ())), preferred_element_type=jnp.float32
+        )
+        factor = gate[at, :]
+        across = jnp.zeros((BLOCK, BLOCK), jnp.float32)
+        for c in range(FF // BLOCK):
+            part = prod[:, c * BLOCK : (c + 1) * BLOCK]
+            cols = pl.ds(c * BLOCK, BLOCK)
+            input_grad[at, cols] = (factor * part).astype(jnp.bfloat16)
+            across = across + rows[at, cols].astype(jnp.float32) * part
+        column = jnp.sum(across, axis=1, keepdims=True)
+        turned = jnp.transpose(jnp.broadcast_to(column, (BLOCK, BLOCK)))
+        gate_grad[pl.ds(block, 1), :] = turned[0:1, :]
+        return 0
+
+    lax.fori_loop(0, ROWS // BLOCK, back, 0)
+    now.sent()
+    gather.finish()
+    for part in after:
+        for k in range(-3, 5):
+            part.arrived(k)
+        part.sent()
+
+
+def last_kernel(
+    rows_next,
+    weight,
+    master,
+    first,
+    second,
+    input_grad,
+    next_out,
+    master_out,
+    first_out,
+    second_out,
+    input_out,
+    out,
+    sems,
+):
+    pairs = (
+        (master, master_out),
+        (first, first_out),
+        (second, second_out),
+        (input_grad, input_out),
+    )
+    stores = [pltpu.make_async_copy(src, dst, sems.at[at]) for at, (src, dst) in enumerate(pairs)]
     for store in stores:
         store.start()
-    after.inplane(0)
-    for chunk in range(CHUNKS):
-        after.forward(chunk)
-    now.out_one()
-    after.inplane(-1)
-    after.inplane(1)
-    after.wait_far()
-    for side in range(2):
-        after.pick_out(side)
-    after.out_two()
-    after.out_one()
-    after.inplane(-2)
-    after.inplane(2)
-    for k in range(-3, 5):
-        now.arrived(k)
+    for block in range(ROWS // BLOCK):
+        at = pl.ds(block * BLOCK, BLOCK)
+        out[at, :] = jnp.dot(
+            rows_next[at, :], weight[...], preferred_element_type=jnp.float32
+        ).astype(jnp.bfloat16)
+        stores.append(
+            pltpu.make_async_copy(out.at[at], next_out.at[at], sems.at[len(pairs) + block])
+        )
+        stores[-1].start()
     for store in stores:
         store.wait()
-    now.sent()
-    gather.finish()
-    for k in range(-3, 5):
-        after.arrived(k)
-    after.sent()
 
 
 ANY = pl.BlockSpec(memory_space=pl.ANY)
+HBM = pl.BlockSpec(memory_space=pltpu.HBM)
 VMEM = pl.BlockSpec(memory_space=pltpu.VMEM)
 SMEM = pl.BlockSpec(memory_space=pltpu.SMEM)
 
 
-def step_call(table, grad, master, moment_one, moment_two):
-    weight = jax.ShapeDtypeStruct((16 * PR, 16 * PC), jnp.bfloat16)
+def in_hbm(x):
+    return pltpu.with_memory_space_constraint(x, pltpu.HBM)
+
+
+def step_call(*operands):
     return pl.pallas_call(
         step_kernel,
         out_shape=(
-            weight,
-            weight,
+            jax.ShapeDtypeStruct((FF, D), jnp.bfloat16),
             jax.ShapeDtypeStruct(STATE, jnp.float32),
             jax.ShapeDtypeStruct(STATE, jnp.bfloat16),
             jax.ShapeDtypeStruct(STATE, jnp.bfloat16),
+            jax.ShapeDtypeStruct((ROWS, FF), jnp.bfloat16),
+            jax.ShapeDtypeStruct((ROWS // BLOCK, BLOCK), jnp.float32),
         ),
-        in_specs=[SMEM, VMEM, ANY, ANY, ANY],
-        out_specs=(VMEM, VMEM, ANY, ANY, ANY),
-        scratch_shapes=SPREAD_SCRATCH * 2 + GATHER_SCRATCH + STATE_SCRATCH,
+        in_specs=[SMEM] * 5 + [VMEM] + [HBM] * 5,
+        out_specs=(VMEM,) * 6,
+        scratch_shapes=sum(SCRATCHES, []) + GATHER_SCRATCH + LOCAL_SCRATCH,
         compiler_params=pltpu.CompilerParams(
-            has_side_effects=True, collective_id=0, vmem_limit_bytes=60 * 2**20
+            has_side_effects=True, collective_id=0, vmem_limit_bytes=STEP_VMEM
         ),
-    )(table, grad, master, moment_one, moment_two)
+    )(*operands)
+
+
+STEP_VMEM = 39 * 2**20
+
+
+def last_call(*operands):
+    shapes = (
+        jax.ShapeDtypeStruct((ROWS, D), jnp.bfloat16),
+        jax.ShapeDtypeStruct(STATE, jnp.float32),
+        jax.ShapeDtypeStruct(STATE, jnp.bfloat16),
+        jax.ShapeDtypeStruct(STATE, jnp.bfloat16),
+        jax.ShapeDtypeStruct((ROWS, FF), jnp.bfloat16),
+    )
+    return pl.pallas_call(
+        last_kernel,
+        out_shape=shapes,
+        in_specs=[VMEM] * 6,
+        out_specs=(ANY,) * 5,
+        scratch_shapes=[pltpu.VMEM((ROWS, D), jnp.bfloat16), pltpu.SemaphoreType.DMA((8,))],
+        compiler_params=pltpu.CompilerParams(vmem_limit_bytes=16 * 2**20),
+    )(*operands)
 
 
 def sum_tables(place, z):
@@ -565,36 +716,26 @@
     moment_one,
     moment_two,
 ):
-    row_count = rows_in.shape[0]
     z = lax.div(lax.axis_index("group"), 2)
-    live_rows = (jnp.arange(row_count, dtype=jnp.int32) < row_counts[0])[:, None]
-    masked_in = jnp.where(live_rows, rows_in, jnp.zeros_like(rows_in))
-    masked_out = jnp.where(live_rows, cotangent, jnp.zeros_like(cotangent))
-    scaled_out = (gate_prob[:, None] * masked_out.astype(jnp.float32)).astype(jnp.bfloat16)
-    slot_grad = lax.dot_general(
-        masked_in, scaled_out, (((0,), (0,)), ((), ())), preferred_element_type=jnp.float32
-    ).astype(jnp.bfloat16)
     old, new = old_place.reshape(-1), new_place.reshape(-1)
-    table = jnp.concatenate([old, *sum_tables(old, z), new])
-    weight, weight_next, new_master, new_first, new_second = step_call(
-        table, slot_grad, master, moment_one, moment_two
-    )
-    back_prod = lax.dot_general(
-        masked_out, weight, (((1,), (1,)), ((), ())), preferred_element_type=jnp.float32
-    )
-    input_grad = (gate_prob[:, None] * back_prod).astype(jnp.bfloat16)
-    gate_grad = jnp.sum(masked_in.astype(jnp.float32) * back_prod, axis=1)
-    next_out = jnp.dot(rows_next, weight_next, preferred_element_type=jnp.float32).astype(
-        jnp.bfloat16
-    )
-    return (
-        input_grad,
-        gate_grad,
-        new_master,
-        new_first,
-        new_second,
-        next_out,
-    )
+    prev, last = sum_tables(old, z)
+    weight_next, new_master, new_first, new_second, input_grad, gate_grad = step_call(
+        in_hbm(old),
+        in_hbm(new),
+        prev,
+        last,
+        row_counts,
+        gate_prob.reshape(ROWS // BLOCK, BLOCK),
+        in_hbm(rows_in),
+        in_hbm(cotangent),
+        in_hbm(master),
+        in_hbm(moment_one),
+        in_hbm(moment_two),
+    )
+    next_out, new_master, new_first, new_second, input_grad = last_call(
+        rows_next, weight_next, new_master, new_first, new_second, input_grad
+    )
+    return (input_grad, gate_grad.reshape(-1), new_master, new_first, new_second, next_out)
 
 
 def solution(mesh):

time: 205 us -> 183 us (0.89)
  matrix products: 12.8 us -> 0 us
  local copies, waits for them, and re-layouts: 8.08 us -> 2.41 us
    dot_general x3 -> x0, matrix products: 12.8 us -> none  [the longest x1 5.55 us: shards(): lax.dot_general(masked_in, scaled_out, (((0,), (0,)), ((), ())), preferre...]
    unnamed x19 -> x6, local copies, waits for them, and re-layouts: 7.45 us -> 1.78 us
    pallas_call x1 -> x2, Pallas kernels: 179 us -> 178 us  [the longest x1 175 us: step_call(): pl.pallas_call(step_kernel, out_shape=(jax.ShapeDtypeStruct((FF, D), jnp....]
where the time goes in v3:
time: 183 us
  Pallas kernels  178 us (97%)
  local copies, waits for them, and re-layouts  2.41 us (1%)
  other arithmetic  1.88 us (1%)
    pallas_call x1, Pallas kernels, step_call(): pl.pallas_call(step_kernel, out_shape=(jax.ShapeDtypeStruct((FF, D), jnp....  175 us

profile of v3, /device:TPU:1, one launch (start us, length us, event | category | flops | bytes accessed | tf_op | source)
XLA Modules:
  0.0 183.2 jit_solution(3177317882453213920)
XLA Ops:
  1.3 0.5 broadcast.39
  1.8 1.3 reduce.16
  3.1 0.1 reshape_reshape.3
  3.3 0.1 reshape_squeeze.7
  3.3 0.1 reshape_squeeze.6
  3.4 0.2 slice_reduce_fusion
  3.6 0.1 add_bitcast_fusion
  3.7 0.1 compare_select_fusion.2
  3.8 0.1 select_reduce_fusion
  4.0 0.1 reduce_max.25
  4.1 0.2 select_reduce_fusion.1
  4.3 0.1 reduce_max.23
  4.4 0.0 copy-start.1
  4.4 0.7 copy-done.1
  5.0 0.0 copy-start
  5.0 174.8 %shard_map.145 = (bf16[768,2048]{1,0:T(8,128)(2,1)S(1)}, f32[64,48,128]{2,1,0:T(8,128)S(1)}, bf16[64,48,128]{2,1,0:T(8,128)(2,1)S(1)}, bf16[64,48,128]{2,1,0:T(8...) custom-call(s32[256]{0:T(256)} %bitcast.19, s32[256]{0:T(256)} %bitcast.20, ...), custom_call_target="tpu_custom_call" | custom-call | tf_op jit(solution)/shard_map/pallas_call | solution.py:646
  179.9 0.0 copy-done
  179.9 2.8 %shard_map.146 = (bf16[512,2048]{1,0:T(8,128)(2,1)}, f32[64,48,128]{2,1,0:T(8,128)}, bf16[64,48,128]{2,1,0:T(8,128)(2,1)}, bf16[64,48,128]{2,1,0:T(8,128)(2,1)}, bf16[512,768]{1,0:T(8,128)(2,1)}) custom-call(bf16[512,768]{1,0:T(8,128)(2,1)S(1)} %copy-done, bf16[768,2048]{1,0:T(8,128)(2,1)S(1)} %get-tuple-element.17.weight, ...), custom_call_target="tpu_custom_call" | custom-call | tf_op jit(solution)/shard_map/pallas_call | solution.py:676
  182.6 0.6 copy.18
  (7 shorter events, 0.1 us)
Async XLA Ops:
  4.4 0.7 copy-start.1
  5.0 174.8 %copy-start = (bf16[512,768]{1,0:T(8,128)(2,1)S(1)}, bf16[512,768]{1,0:T(8,128)(2,1)}, u32[]{:S(2)}) copy-start(bf16[512,768]{1,0:T(8,128)(2,1)} %rows_next.1) | copy-start | bytes 2359300

commit v4 on v3

--- a/solution.py
+++ b/solution.py
@@ -64,18 +64,22 @@
 
 
 def meet():
-    z, i, _, _ = my_place()
+    z, _, g, s = my_place()
     barrier = pltpu.get_barrier_semaphore()
-
-    def go(n, _):
-        m = PEERS - n
-        k = lax.div(m, INPLANE)
-        plane = lax.rem(z + k + 3 * lax.div(k, 3), PLANES)
-        g, s = device_at(plane, lax.rem(i + m, INPLANE))
-        pl.semaphore_signal(barrier, inc=1, device_id=(g, s), device_id_type=MESH)
-        return 0
-
-    lax.fori_loop(0, PEERS, go, 0)
+    for k in (2, -2, 1, -1, 0):
+        for half in range(2):
+            group = plane_at(z, k) * 2 + lax.rem(g + half, 2)
+
+            def go(j, _, group=group):
+                pl.semaphore_signal(
+                    barrier,
+                    inc=1,
+                    device_id=(group, lax.rem(s + j, 16)),
+                    device_id_type=MESH,
+                )
+                return 0
+
+            lax.fori_loop(1 if (k, half) == (0, 0) else 0, 16, go, 0)
     return barrier
 
 
@@ -224,9 +228,49 @@
     ]
 
 
+def build_tables(old, tab):
+    z, _, _, _ = my_place()
+    lanes = lax.broadcasted_iota(jnp.int32, (8, 128), 1)
+
+    def near(t, lists):
+        out = []
+        for value, k in zip(lists, (-1, 1)):
+            value = jnp.where(lanes == t, old[z * INPLANE + t], value)
+            out.append(jnp.where(lanes == 32 + t, old[plane_at(z, k) * INPLANE + t], value))
+        return tuple(out)
+
+    def far(t, lists):
+        out = []
+        for core, (value, k) in enumerate(zip(lists, (-2, 2))):
+            expert = old[plane_at(z, k) * INPLANE + 2 * t + core]
+            out.append(jnp.where(lanes == 64 + t, expert, value))
+        return tuple(out)
+
+    none = jnp.full((8, 128), -1, jnp.int32)
+    lists = lax.fori_loop(0, 16, far, lax.fori_loop(0, INPLANE, near, (none, none)))
+    at = lax.broadcasted_iota(jnp.int32, (128, 128), 0)
+    across = lax.broadcasted_iota(jnp.int32, (128, 128), 1)
+
+    def put(row, found):
+        value = jnp.where(found, at, -1)
+        size = 128
+        while size > 1:
+            size //= 2
+            value = jnp.maximum(value[:size], value[size:])
+        tab[row : row + 1, :] = jnp.where(value < 0, FAR, value)
+
+    for side in range(2):
+        wide = jnp.broadcast_to(lists[side][0:1, :], (128, 128))
+        tall = jnp.transpose(wide)
+        put(side, (tall == wide) & (at < across))
+        put(2 + side, tall == across)
+        if side == 0:
+            put(4, (tall == across) & (at < INPLANE))
+
+
 class Gather:
-    def __init__(self, prev, last, grad, met0, met1, met2, sums, parts, sems, part_sems):
-        self.prev, self.last, self.grad = prev, last, grad
+    def __init__(self, tab, grad, met0, met1, met2, sums, parts, sems, part_sems):
+        self.tab, self.grad = tab, grad
         self.met0, self.met1, self.met2 = met0, met1, met2
         self.sums = sums
         self.parts = parts
@@ -308,14 +352,14 @@
 
     def chain(self, value_at, count, side):
         def step(t, _):
-            before = self.sums[self.prev[side * FAR + t]]
+            before = self.sums[self.tab[side, t]]
             self.sums[t] = before + value_at(t).astype(jnp.float32)
             return 0
 
         lax.fori_loop(0, count, step, 0)
 
     def summed(self, which, e):
-        return self.sums[self.last[which * EXPERTS + e]]
+        return self.sums[self.tab[2 + which, e]]
 
     def clear(self):
         self.sums[...] = jnp.zeros_like(self.sums)
@@ -363,7 +407,7 @@
     def total(self, e, rows):
         value = self.parts[3][0, e, rows].astype(jnp.float32)
         value = value + self.parts[3][1, e, rows].astype(jnp.float32)
-        return value + self.sums[self.last[2 * EXPERTS + e], rows]
+        return value + self.sums[self.tab[4, e], rows]
 
     def finish(self):
         take(self.met2.at[0], self.out_sem)
@@ -398,6 +442,7 @@
 LOCAL_SCRATCH = [
     pltpu.VMEM(STATE, jnp.bfloat16),
     *[pltpu.VMEM((EXPERTS, rows, PC), jnp.bfloat16) for _, rows in PARTS],
+    pltpu.VMEM((ROWS // BLOCK, BLOCK), jnp.float32),
     pltpu.VMEM((FF, D), jnp.bfloat16),
     pltpu.VMEM((FF, D), jnp.bfloat16),
     pltpu.VMEM((ROWS, FF), jnp.bfloat16),
@@ -405,7 +450,9 @@
     pltpu.VMEM((ROWS, D), jnp.bfloat16),
     pltpu.VMEM((ROWS, D), jnp.bfloat16),
     pltpu.VMEM((ROWS, BLOCK), jnp.float32),
-    pltpu.SemaphoreType.DMA((5,)),
+    pltpu.SemaphoreType.DMA((7,)),
+    pltpu.VMEM((8, 128), jnp.int32),
+    pltpu.SMEM((8, 128), jnp.int32),
 ]
 
 
@@ -414,10 +461,8 @@
 def step_kernel(
     old,
     new,
-    prev,
-    last,
     count,
-    gate_in,
+    gate_hbm,
     rows_in,
     cot_in,
     master_in,
@@ -433,29 +478,32 @@
 ):
     n = len(SCRATCHES[0])
     m = len(GATHER_SCRATCH)
-    own, own_a, own_b, grad, weight, rows, rows_t, cot, scaled, gate, load_sems = scratch[3 * n + m :]
+    own, own_a, own_b, gate_in, grad, weight, rows, rows_t, cot, scaled, gate, load_sems, tab, tab_smem = (
+        scratch[3 * n + m :]
+    )
     now = Spread(old, own, weight, 0, CHUNKS, scratch[0:n])
     after = [
         Spread(new, part, weight_next, PARTS[at][0], 1, scratch[(at + 1) * n : (at + 2) * n])
         for at, part in enumerate((own_a, own_b))
     ]
     rest = scratch[3 * n : 3 * n + m]
-    gather = Gather(prev, last, grad, *rest[0:4], rest[4:8], *rest[8:])
+    gather = Gather(tab_smem, grad, *rest[0:4], rest[4:8], *rest[8:])
     z = now.z
 
+    barrier = meet()
     pairs = (
         (master_in, master),
         (rows_in, rows),
         (cot_in, cot),
         (first_in, first),
         (second_in, second),
+        (gate_hbm, gate_in),
     )
     loads = [
         pltpu.make_async_copy(src, dst, load_sems.at[at]) for at, (src, dst) in enumerate(pairs)
     ]
     for load in loads:
         load.start()
-    barrier = meet()
     loads[0].wait()
 
     def cast(e, _):
@@ -468,8 +516,10 @@
         now.start_own(chunk)
 
     now.inplane(0)
+    build_tables(old, tab)
     loads[1].wait()
     loads[2].wait()
+    loads[5].wait()
     live_count = count[0]
     for block in range(ROWS // BLOCK):
         at = pl.ds(block * BLOCK, BLOCK)
@@ -507,6 +557,9 @@
     gather.clear()
     gather.start_far()
     gather.start_inplane(2)
+    tables = pltpu.make_async_copy(tab, tab_smem, load_sems.at[6])
+    tables.start()
+    tables.wait()
     now.forward(0)
     now.forward(1)
     for side in range(2):
@@ -526,7 +579,7 @@
     now.inplane(-2)
     now.inplane(2)
     gather.level_zero()
-    for load in loads[3:]:
+    for load in loads[3:5]:
         load.wait()
 
     def update(e, rows, own_next):
@@ -602,11 +655,13 @@
     first,
     second,
     input_grad,
+    gate_grad,
     next_out,
     master_out,
     first_out,
     second_out,
     input_out,
+    gate_out,
     out,
     sems,
 ):
@@ -615,6 +670,7 @@
         (first, first_out),
         (second, second_out),
         (input_grad, input_out),
+        (gate_grad, gate_out),
     )
     stores = [pltpu.make_async_copy(src, dst, sems.at[at]) for at, (src, dst) in enumerate(pairs)]
     for store in stores:
@@ -653,7 +709,7 @@
             jax.ShapeDtypeStruct((ROWS, FF), jnp.bfloat16),
             jax.ShapeDtypeStruct((ROWS // BLOCK, BLOCK), jnp.float32),
         ),
-        in_specs=[SMEM] * 5 + [VMEM] + [HBM] * 5,
+        in_specs=[SMEM] * 3 + [HBM] * 6,
         out_specs=(VMEM,) * 6,
         scratch_shapes=sum(SCRATCHES, []) + GATHER_SCRATCH + LOCAL_SCRATCH,
         compiler_params=pltpu.CompilerParams(
@@ -672,36 +728,16 @@
         jax.ShapeDtypeStruct(STATE, jnp.bfloat16),
         jax.ShapeDtypeStruct(STATE, jnp.bfloat16),
         jax.ShapeDtypeStruct((ROWS, FF), jnp.bfloat16),
+        jax.ShapeDtypeStruct((ROWS // BLOCK, BLOCK), jnp.float32),
     )
     return pl.pallas_call(
         last_kernel,
         out_shape=shapes,
-        in_specs=[VMEM] * 6,
-        out_specs=(ANY,) * 5,
-        scratch_shapes=[pltpu.VMEM((ROWS, D), jnp.bfloat16), pltpu.SemaphoreType.DMA((8,))],
+        in_specs=[VMEM] * 7,
+        out_specs=(ANY,) * 6,
+        scratch_shapes=[pltpu.VMEM((ROWS, D), jnp.bfloat16), pltpu.SemaphoreType.DMA((9,))],
         compiler_params=pltpu.CompilerParams(vmem_limit_bytes=16 * 2**20),
     )(*operands)
-
-
-def sum_tables(place, z):
-    planes = place.reshape(PLANES, INPLANE)
-    around = lax.dynamic_slice(
-        jnp.concatenate([planes, planes], 0), (lax.rem(z + 6, PLANES), 0), (5, INPLANE)
-    )
-    up = jnp.concatenate([around[2], around[1], around[0].reshape(16, 2)[:, 0]])
-    down = jnp.concatenate([around[2], around[3], around[4].reshape(16, 2)[:, 1]])
-    both = jnp.stack([up, down])
-    at = jnp.arange(FAR, dtype=jnp.int32)
-    same = both[:, :, None] == both[:, None, :]
-    earlier = at[None, :] < at[:, None]
-    prev = jnp.max(jnp.where(same & earlier[None], at[None, None, :], -1), axis=2)
-    prev = jnp.where(prev < 0, FAR, prev)
-    lists = jnp.stack([up, down, jnp.where(at < INPLANE, up, -1)])
-    ids = jnp.arange(EXPERTS, dtype=jnp.int32)
-    found = lists[:, None, :] == ids[None, :, None]
-    last = jnp.max(jnp.where(found, at[None, None, :], -1), axis=2)
-    last = jnp.where(last < 0, FAR, last)
-    return prev.reshape(-1), last.reshape(-1)
 
 
 def shards(
@@ -716,24 +752,20 @@
     moment_one,
     moment_two,
 ):
-    z = lax.div(lax.axis_index("group"), 2)
     old, new = old_place.reshape(-1), new_place.reshape(-1)
-    prev, last = sum_tables(old, z)
     weight_next, new_master, new_first, new_second, input_grad, gate_grad = step_call(
         in_hbm(old),
         in_hbm(new),
-        prev,
-        last,
         row_counts,
-        gate_prob.reshape(ROWS // BLOCK, BLOCK),
+        in_hbm(gate_prob.reshape(ROWS // BLOCK, BLOCK)),
         in_hbm(rows_in),
         in_hbm(cotangent),
         in_hbm(master),
         in_hbm(moment_one),
         in_hbm(moment_two),
     )
-    next_out, new_master, new_first, new_second, input_grad = last_call(
-        rows_next, weight_next, new_master, new_first, new_second, input_grad
+    next_out, new_master, new_first, new_second, input_grad, gate_grad = last_call(
+        rows_next, weight_next, new_master, new_first, new_second, input_grad, gate_grad
     )
     return (input_grad, gate_grad.reshape(-1), new_master, new_first, new_second, next_out)
 

time: 183 us -> 178 us (0.973)
  local copies, waits for them, and re-layouts: 2.41 us -> 0.01 us
  other arithmetic: 1.88 us -> 0 us
where the time goes in v4:
time: 178 us
  Pallas kernels  177 us (99%)
    pallas_call x1, Pallas kernels, step_call(): pl.pallas_call(step_kernel, out_shape=(jax.ShapeDtypeStruct((FF, D), jnp....  174 us

profile of v4, /device:TPU:1, one launch (start us, length us, event | category | flops | bytes accessed | tf_op | source)
XLA Modules:
  0.0 178.0 jit_solution(12076590682862055403)
XLA Ops:
  1.3 0.0 copy-start
  1.3 173.9 %shard_map.145 = (bf16[768,2048]{1,0:T(8,128)(2,1)S(1)}, f32[64,48,128]{2,1,0:T(8,128)S(1)}, bf16[64,48,128]{2,1,0:T(8,128)(2,1)S(1)}, bf16[64,48,128]{2,1,0:T(8...) custom-call(s32[256]{0:T(256)} %bitcast.5, s32[256]{0:T(256)} %bitcast.6, s32[1]{0:T(128)S(6)} %copy.16.count, ...), custom_call_target="tpu_custom_call" | custom-call | tf_op jit(solution)/shard_map/pallas_call | solution.py:702
  175.2 0.0 copy-done
  175.2 2.8 %shard_map.146 = (bf16[512,2048]{1,0:T(8,128)(2,1)}, f32[64,48,128]{2,1,0:T(8,128)}, bf16[64,48,128]{2,1,0:T(8,128)(2,1)}, bf16[64,48,128]{2,1,0:T(8,128)(2,1)},...) custom-call(bf16[512,768]{1,0:T(8,128)(2,1)S(1)} %copy-done, bf16[768,2048]{1,0:T(8,128)(2,1)S(1)} %get-tuple-element.18.weight, ...), custom_call_target="tpu_custom_call" | custom-call | tf_op jit(solution)/shard_map/pallas_call | solution.py:733
Async XLA Ops:
  1.3 174.0 %copy-start = (bf16[512,768]{1,0:T(8,128)(2,1)S(1)}, bf16[512,768]{1,0:T(8,128)(2,1)}, u32[]{:S(2)}) copy-start(bf16[512,768]{1,0:T(8,128)(2,1)} %rows_next.1) | copy-start | bytes 2359300

commit v5 on v4

--- a/solution.py
+++ b/solution.py
@@ -34,6 +34,18 @@
 
 def device_at(plane, i):
     return (plane * 2 + lax.div(i, 16), lax.rem(i, 16))
+
+
+def each(count, go, first=0):
+    _, _, g, s = my_place()
+    for half in range(2):
+        xlo = lax.rem(g + half, 2)
+
+        def step(j, _, half=half, xlo=xlo):
+            go(16 * half + j, xlo, lax.rem(s + j, 16))
+            return 0
+
+        lax.fori_loop(first if half == 0 else 0, count, step, 0)
 
 
 def shard_slice(ref, block_row, block_col):
@@ -59,6 +71,7 @@
 
 
 CHUNKS = 4
+EARLY = 3
 PARTS = ((0, 32), (32, 16))
 PEERS = 5 * INPLANE - 1
 
@@ -93,8 +106,8 @@
         self.z, self.i, self.g, self.s = my_place()
         self.xlo = lax.rem(self.g, 2)
 
-    def expert(self, plane, t):
-        return self.place[plane * INPLANE + t]
+    def expert(self, plane, xlo, s):
+        return self.place[plane * INPLANE + xlo * 16 + s]
 
     def ring(self, src, dst, hop, side, chunk):
         part = pl.ds(chunk * self.step, self.step)
@@ -129,81 +142,81 @@
         return self.weight.at[self.span(), pl.ds(pl.multiple_of(column * PC, PC), PC)]
 
     def inplane(self, k):
-        z, i = self.z, self.i
+        z = self.z
         ref = {0: self.own, -1: self.near[0], 1: self.near[1], -2: self.far[0], 2: self.far[1]}[k]
         base = {0: 0, -1: 32, 1: 64, -2: 192, 2: 224}[k]
         column = plane_at(z, k) * 2 + self.xlo
 
-        def pick(j, _):
-            t = lax.rem(i + j, INPLANE)
-            self.picks[base + j] = ref[self.expert(z, t)]
-            return 0
-
-        def go(j, _):
-            t = lax.rem(i + j, INPLANE)
+        def pick(n, xlo, s):
+            self.picks[base + n] = ref[self.expert(z, xlo, s)]
+
+        def go(n, xlo, s):
             send(
-                self.picks.at[base + j],
+                self.picks.at[base + n],
                 self.target(column),
                 self.out_sem,
                 self.in_sems.at[k + 3],
-                device_at(z, t),
+                (z * 2 + xlo, s),
             )
-            return 0
-
-        lax.fori_loop(0, INPLANE, pick, 0)
-        lax.fori_loop(1, INPLANE, go, 0)
+
+        each(16, pick)
+        each(16, go, 1)
         self.weight[self.span(), pl.ds(pl.multiple_of(column * PC, PC), PC)] = self.picks[base]
 
-    def other(self, side, j):
-        return lax.rem((lax.div(self.i, 2) + j) * 2, INPLANE) + side
+    def others(self, go):
+        _, _, g, s = my_place()
+        for half in range(2):
+            xlo = lax.rem(g + half, 2)
+
+            def step(j, _, half=half, xlo=xlo):
+                go(8 * half + j, xlo, lax.rem(s - lax.rem(s, 2) + 2 * j, 16))
+                return 0
+
+            lax.fori_loop(0, 8, step, 0)
 
     def pick_out(self, side):
         ref, base = self.far[side], 96 + 48 * side
         sign = 1 - 2 * side
         one, two = plane_at(self.z, sign), plane_at(self.z, 2 * sign)
 
-        def pick_two(j, _):
-            self.picks[base + 32 + j] = ref[self.expert(two, self.other(side, j))]
-            return 0
-
-        def pick_one(j, _):
-            self.picks[base + j] = ref[self.expert(one, lax.rem(self.i + j, INPLANE))]
-            return 0
-
-        lax.fori_loop(0, 16, pick_two, 0)
-        lax.fori_loop(0, INPLANE, pick_one, 0)
+        def pick_two(n, xlo, s):
+            self.picks[base + 32 + n] = ref[self.expert(two, xlo, s + side)]
+
+        def pick_one(n, xlo, s):
+            self.picks[base + n] = ref[self.expert(one, xlo, s)]
+
+        self.others(pick_two)
+        each(16, pick_one)
 
     def out_two(self):
-        def go_two(j, _):
+        def go_two(n, xlo, s):
             for side in range(2):
                 sign = 1 - 2 * side
                 column = plane_at(self.z, -2 * sign) * 2 + self.xlo
                 send(
-                    self.picks.at[96 + 48 * side + 32 + j],
+                    self.picks.at[96 + 48 * side + 32 + n],
                     self.target(column),
                     self.out_sem,
                     self.in_sems.at[7],
-                    device_at(plane_at(self.z, 2 * sign), self.other(side, j)),
+                    (plane_at(self.z, 2 * sign) * 2 + xlo, s + side),
                 )
-            return 0
-
-        lax.fori_loop(0, 16, go_two, 0)
+
+        self.others(go_two)
 
     def out_one(self):
-        def go_one(j, _):
+        def go_one(n, xlo, s):
             for side in range(2):
                 sign = 1 - 2 * side
                 column = plane_at(self.z, -2 * sign) * 2 + self.xlo
                 send(
-                    self.picks.at[96 + 48 * side + j],
+                    self.picks.at[96 + 48 * side + n],
                     self.target(column),
                     self.out_sem,
                     self.in_sems.at[3 - 3 * sign],
-                    device_at(plane_at(self.z, sign), lax.rem(self.i + j, INPLANE)),
+                    (plane_at(self.z, sign) * 2 + xlo, s),
                 )
-            return 0
-
-        lax.fori_loop(0, INPLANE, go_one, 0)
+
+        each(16, go_one)
 
     def arrived(self, k):
         count = 31 if -2 <= k <= 2 else 32
@@ -278,8 +291,8 @@
         self.z, self.i, self.g, self.s = my_place()
         self.out_sem = sems.at[0]
 
-    def piece(self, plane, t):
-        return shard_slice(self.grad, lax.rem(t, 16), plane * 2 + lax.div(t, 16))
+    def piece(self, plane, xlo, s):
+        return shard_slice(self.grad, s, plane * 2 + xlo)
 
     def piece_value(self, plane, t):
         rows = pl.ds(pl.multiple_of(lax.rem(t, 16) * PR, 16), PR)
@@ -292,77 +305,74 @@
         two = lax.rem(z + 2 + 4 * core, PLANES)
         opposite = plane_at(z, 4)
 
-        def go_two(j, _):
-            t = lax.rem(i + j, INPLANE)
+        def go_two(n, xlo, s):
             send(
-                self.piece(opposite, t),
+                self.piece(opposite, xlo, s),
                 self.met2.at[core, 64 + lax.div(i, 2)],
                 self.out_sem,
                 self.sems.at[4 + core],
-                device_at(two, t),
+                (two * 2 + xlo, s),
             )
-            return 0
-
-        def go_one(j, _):
-            t = lax.rem(i + j, INPLANE)
+
+        def go_one(n, xlo, s):
             for side in range(2):
                 sign = 1 - 2 * side
                 send(
-                    self.piece(plane_at(z, 3 * sign), t),
+                    self.piece(plane_at(z, 3 * sign), xlo, s),
                     self.met2.at[side, 32 + i],
                     self.out_sem,
                     self.sems.at[4 + side],
-                    device_at(plane_at(z, sign), t),
+                    (plane_at(z, sign) * 2 + xlo, s),
                 )
-            return 0
-
-        lax.fori_loop(0, INPLANE, go_two, 0)
-        lax.fori_loop(0, INPLANE, go_one, 0)
+
+        each(16, go_two)
+        each(16, go_one)
 
     def start_inplane(self, level):
         z, i = self.z, self.i
 
-        def go(level, j):
-            t = lax.rem(i + j, INPLANE)
+        def go(n, xlo, s):
             for side in range(2):
                 sign = 1 - 2 * side
                 met = self.met2 if level == 2 else self.met1
                 send(
-                    self.piece(plane_at(z, level * sign), t),
+                    self.piece(plane_at(z, level * sign), xlo, s),
                     met.at[side, i],
                     self.out_sem,
                     self.sems.at[2 * level + side],
-                    device_at(z, t),
+                    (z * 2 + xlo, s),
                 )
-            return 0
-
-        def go_own(j, _):
-            t = lax.rem(i + j, INPLANE)
-            send(self.piece(z, t), self.met0.at[i], self.out_sem, self.sems.at[1], device_at(z, t))
-            return 0
+
+        def go_own(n, xlo, s):
+            send(
+                self.piece(z, xlo, s),
+                self.met0.at[i],
+                self.out_sem,
+                self.sems.at[1],
+                (z * 2 + xlo, s),
+            )
 
         if level == 0:
-            lax.fori_loop(1, INPLANE, go_own, 0)
+            each(16, go_own, 1)
             self.met0[i] = self.piece_value(z, i)
             return
-        lax.fori_loop(1, INPLANE, lambda j, _: go(level, j), 0)
+        each(16, go, 1)
         met = self.met2 if level == 2 else self.met1
         for side in range(2):
             met[side, i] = self.piece_value(plane_at(z, level * (1 - 2 * side)), i)
 
-    def chain(self, value_at, count, side):
+    def chain(self, value_at, count, row, sides):
         def step(t, _):
-            before = self.sums[self.tab[side, t]]
-            self.sums[t] = before + value_at(t).astype(jnp.float32)
+            for side in range(sides):
+                before = self.sums[side][self.tab[row * side, t]]
+                self.sums[side][t] = before + value_at(side, t).astype(jnp.float32)
             return 0
 
         lax.fori_loop(0, count, step, 0)
 
-    def summed(self, which, e):
-        return self.sums[self.tab[2 + which, e]]
-
     def clear(self):
-        self.sums[...] = jnp.zeros_like(self.sums)
+        for sums in self.sums:
+            sums[...] = jnp.zeros_like(sums)
 
     def pass_on(self, level, side):
         sign = 1 - 2 * side
@@ -374,40 +384,49 @@
             device_at(plane_at(self.z, sign), self.i),
         )
 
-    def level_two(self, side):
-        take(self.met2.at[side, pl.ds(0, FAR - 1)], self.sems.at[4 + side])
-        self.chain(lambda t: self.met2[side, t], FAR, side)
+    def level_two(self):
+        for side in range(2):
+            take(self.met2.at[side, pl.ds(0, FAR - 1)], self.sems.at[4 + side])
+        self.chain(lambda side, t: self.met2[side, t], FAR, 1, 2)
 
         def put(e, _):
-            self.parts[0][side, e] = self.summed(side, e).astype(jnp.bfloat16)
+            for side in range(2):
+                value = self.sums[side][self.tab[2 + side, e]]
+                self.parts[0][side, e] = value.astype(jnp.bfloat16)
             return 0
 
         lax.fori_loop(0, EXPERTS, put, 0)
-        self.pass_on(0, side)
-
-    def level_one(self, side):
-        take(self.met1.at[side, pl.ds(0, INPLANE - 1)], self.sems.at[2 + side])
-        self.chain(lambda t: self.met1[side, t], INPLANE, 0)
-        take(self.parts[2].at[side], self.part_sems.at[1, 0, side])
+        for side in range(2):
+            self.pass_on(0, side)
+
+    def level_one(self):
+        for side in range(2):
+            take(self.met1.at[side, pl.ds(0, INPLANE - 1)], self.sems.at[2 + side])
+        self.chain(lambda side, t: self.met1[side, t], INPLANE, 0, 2)
+        for side in range(2):
+            take(self.parts[2].at[side], self.part_sems.at[1, 0, side])
 
         def put(e, _):
-            value = self.summed(2, e) + self.parts[2][side, e].astype(jnp.float32)
-            self.parts[1][side, e] = value.astype(jnp.bfloat16)
+            for side in range(2):
+                value = self.sums[side][self.tab[4, e]]
+                value = value + self.parts[2][side, e].astype(jnp.float32)
+                self.parts[1][side, e] = value.astype(jnp.bfloat16)
             return 0
 
         lax.fori_loop(0, EXPERTS, put, 0)
-        self.pass_on(1, side)
+        for side in range(2):
+            self.pass_on(1, side)
 
     def level_zero(self):
         take(self.met0.at[pl.ds(0, INPLANE - 1)], self.sems.at[1])
-        self.chain(lambda t: self.met0[t], INPLANE, 0)
+        self.chain(lambda _, t: self.met0[t], INPLANE, 0, 1)
         for side in range(2):
             take(self.parts[3].at[side], self.part_sems.at[1, 1, side])
 
     def total(self, e, rows):
         value = self.parts[3][0, e, rows].astype(jnp.float32)
         value = value + self.parts[3][1, e, rows].astype(jnp.float32)
-        return value + self.sums[self.tab[4, e], rows]
+        return value + self.sums[0][self.tab[4, e], rows]
 
     def finish(self):
         take(self.met2.at[0], self.out_sem)
@@ -423,6 +442,7 @@
     pltpu.VMEM((INPLANE, PR, PC), jnp.bfloat16),
     pltpu.VMEM((2, INPLANE, PR, PC), jnp.bfloat16),
     pltpu.VMEM((2, FAR, PR, PC), jnp.bfloat16),
+    pltpu.VMEM((FAR + 1, PR, PC), jnp.float32),
     pltpu.VMEM((FAR + 1, PR, PC), jnp.float32),
     pltpu.VMEM((2, EXPERTS, PR, PC), jnp.bfloat16),
     pltpu.VMEM((2, EXPERTS, PR, PC), jnp.bfloat16),
@@ -487,7 +507,7 @@
         for at, part in enumerate((own_a, own_b))
     ]
     rest = scratch[3 * n : 3 * n + m]
-    gather = Gather(tab_smem, grad, *rest[0:4], rest[4:8], *rest[8:])
+    gather = Gather(tab_smem, grad, *rest[0:3], rest[3:5], rest[5:9], *rest[9:])
     z = now.z
 
     barrier = meet()
@@ -512,7 +532,7 @@
 
     lax.fori_loop(0, EXPERTS, cast, 0)
     pl.semaphore_wait(barrier, PEERS)
-    for chunk in range(CHUNKS):
+    for chunk in range(EARLY):
         now.start_own(chunk)
 
     now.inplane(0)
@@ -556,22 +576,22 @@
     lax.fori_loop(0, PLANES, slot_grad, 0)
     gather.clear()
     gather.start_far()
+    for chunk in range(EARLY, CHUNKS):
+        now.start_own(chunk)
     gather.start_inplane(2)
     tables = pltpu.make_async_copy(tab, tab_smem, load_sems.at[6])
     tables.start()
     tables.wait()
     now.forward(0)
     now.forward(1)
-    for side in range(2):
-        gather.level_two(side)
+    gather.level_two()
     gather.start_inplane(1)
     gather.start_inplane(0)
     now.forward(2)
     now.forward(3)
     now.inplane(-1)
     now.inplane(1)
-    for side in range(2):
-        gather.level_one(side)
+    gather.level_one()
     now.wait_far()
     for side in range(2):
         now.pick_out(side)
@@ -718,7 +738,7 @@
     )(*operands)
 
 
-STEP_VMEM = 39 * 2**20
+STEP_VMEM = 41 * 2**20
 
 
 def last_call(*operands):

time: 178 us -> 176 us (0.989)
  Pallas kernels: 177 us -> 174 us
    pallas_call x1, Pallas kernels: 174 us -> 172 us  [step_call(): pl.pallas_call(step_kernel, out_shape=(jax.ShapeDtypeStruct((FF, D), jnp....]
where the time goes in v5:
time: 176 us
  Pallas kernels  174 us (99%)
    pallas_call x1, Pallas kernels, step_call(): pl.pallas_call(step_kernel, out_shape=(jax.ShapeDtypeStruct((FF, D), jnp....  172 us

profile of v5, /device:TPU:1, one launch (start us, length us, event | category | flops | bytes accessed | tf_op | source)
XLA Modules:
  0.0 175.6 jit_solution(15403364666337597260)
XLA Ops:
  1.3 0.0 copy-start
  1.3 171.5 %shard_map.145 = (bf16[768,2048]{1,0:T(8,128)(2,1)S(1)}, f32[64,48,128]{2,1,0:T(8,128)S(1)}, bf16[64,48,128]{2,1,0:T(8,128)(2,1)S(1)}, bf16[64,48,128]{2,1,0:T(8...) custom-call(s32[256]{0:T(256)} %bitcast.5, s32[256]{0:T(256)} %bitcast.6, s32[1]{0:T(128)S(6)} %copy.16.count, ...), custom_call_target="tpu_custom_call" | custom-call | tf_op jit(solution)/shard_map/pallas_call | solution.py:722
  172.8 0.0 copy-done
  172.9 2.8 %shard_map.146 = (bf16[512,2048]{1,0:T(8,128)(2,1)}, f32[64,48,128]{2,1,0:T(8,128)}, bf16[64,48,128]{2,1,0:T(8,128)(2,1)}, bf16[64,48,128]{2,1,0:T(8,128)(2,1)},...) custom-call(bf16[512,768]{1,0:T(8,128)(2,1)S(1)} %copy-done, bf16[768,2048]{1,0:T(8,128)(2,1)S(1)} %get-tuple-element.18.weight, ...), custom_call_target="tpu_custom_call" | custom-call | tf_op jit(solution)/shard_map/pallas_call | solution.py:753
Async XLA Ops:
  1.3 171.6 %copy-start = (bf16[512,768]{1,0:T(8,128)(2,1)S(1)}, bf16[512,768]{1,0:T(8,128)(2,1)}, u32[]{:S(2)}) copy-start(bf16[512,768]{1,0:T(8,128)(2,1)} %rows_next.1) | copy-start | bytes 2359300
